TPU v7x, 16 devices: a whole 2x2x2 slice. The times are simulated.
16 devices in a mesh: dp: 4 (over z, y), ep: 4 (over x, core).
Axes of the slice: x: 2, y: 2, z: 2, core: 2. Of those that a mesh axis runs over, the one named last changes fastest.
Arguments:
- x_in: bfloat16 [32768, 512], P(('dp', 'ep')), parts along dimension 0
- grad_y: bfloat16 [32768, 512], P(('dp', 'ep')), parts along dimension 0
- ids_a: int32 [32768, 2], P(('dp', 'ep')), parts along dimension 0
- gate_a: float32 [32768, 2], P(('dp', 'ep')), parts along dimension 0
- ids_b: int32 [32768, 2], P(('dp', 'ep')), parts along dimension 0
- gate_b: float32 [32768, 2], P(('dp', 'ep')), parts along dimension 0
- w1_a: bfloat16 [8, 512, 1792], P('ep')
- w3_a: bfloat16 [8, 512, 1792], P('ep')
- w2_a: bfloat16 [8, 1792, 512], P('ep')
- w1_b: bfloat16 [8, 512, 1792], P('ep')
- w3_b: bfloat16 [8, 512, 1792], P('ep')
- w2_b: bfloat16 [8, 1792, 512], P('ep')
- wg_mid: bfloat16 [512, 1792], replicated
- wu_mid: bfloat16 [512, 1792], replicated
- wd_mid: bfloat16 [1792, 512], replicated
- wg_top: bfloat16 [512, 1792], replicated
- wu_top: bfloat16 [512, 1792], replicated
- wd_top: bfloat16 [1792, 512], replicated
Outputs:
- output 1: bfloat16 [32768, 512], P(('dp', 'ep')), parts along dimension 0
- output 2: bfloat16 [32768, 512], P(('dp', 'ep')), parts along dimension 0
- output 3: float32 [32, 512, 1792], P(('dp', 'ep')), parts along dimension 0
- output 4: float32 [32, 512, 1792], P(('dp', 'ep')), parts along dimension 0
- output 5: float32 [32, 1792, 512], P(('dp', 'ep')), parts along dimension 0
- output 6: float32 [32, 512, 1792], P(('dp', 'ep')), parts along dimension 0
- output 7: float32 [32, 512, 1792], P(('dp', 'ep')), parts along dimension 0
- output 8: float32 [32, 1792, 512], P(('dp', 'ep')), parts along dimension 0
- output 9: float32 [32768, 2], P(('dp', 'ep')), parts along dimension 0
- output 10: float32 [32768, 2], P(('dp', 'ep')), parts along dimension 0
There are 4 independent parts. A program takes and returns all parts, laid end to end along the dimension named above; an argument that names none is the same for every part.
All inputs are finite; a program needn't handle non-finite values.
Results may differ from a plain program's by a relative error of at most 0.02.
Values are sent between devices in bfloat16 or wider.
A program may use at most 1 GiB of HBM per device.

v0:
```python
import jax
import jax.numpy as jnp
from jax import lax
from jax.sharding import PartitionSpec as P

CONTRACT_LAST = (((1,), (1,)), ((), ()))


def route_pairs(expert_ids, n_exp, capacity):
    n_tok, top_k = expert_ids.shape
    flat_ids = expert_ids.reshape(-1)
    onehot = (flat_ids[:, None] == jnp.arange(n_exp, dtype=jnp.int32)[None, :]).astype(jnp.int32)
    slots = jnp.sum((jnp.cumsum(onehot, axis=0) - onehot) * onehot, axis=1)
    pair_rows = flat_ids * capacity + slots
    filler = jnp.full((n_exp * capacity,), n_tok * top_k, jnp.int32)
    filler = filler.at[pair_rows].set(jnp.arange(n_tok * top_k, dtype=jnp.int32))
    return pair_rows, filler


def swiglu_grad(pre_gate, pre_up, grad_hidden):
    sigma = jax.nn.sigmoid(pre_gate)
    grad_gate = grad_hidden * pre_up * sigma * (1.0 + pre_gate * (1.0 - sigma))
    grad_up = grad_hidden * pre_gate * sigma
    return grad_gate.astype(jnp.bfloat16), grad_up.astype(jnp.bfloat16)


def dense_forward(x_rows, w_gate, w_up, w_down):
    pre_gate = jnp.dot(x_rows, w_gate, preferred_element_type=jnp.float32)
    pre_up = jnp.dot(x_rows, w_up, preferred_element_type=jnp.float32)
    hidden = (jax.nn.silu(pre_gate) * pre_up).astype(jnp.bfloat16)
    branch = jnp.dot(hidden, w_down, preferred_element_type=jnp.float32)
    return (x_rows.astype(jnp.float32) + branch).astype(jnp.bfloat16)


def dense_backward(x_rows, grad_out, w_gate, w_up, w_down):
    pre_gate = jnp.dot(x_rows, w_gate, preferred_element_type=jnp.float32)
    pre_up = jnp.dot(x_rows, w_up, preferred_element_type=jnp.float32)
    grad_hidden = lax.dot_general(grad_out, w_down, CONTRACT_LAST, preferred_element_type=jnp.float32)
    grad_gate, grad_up = swiglu_grad(pre_gate, pre_up, grad_hidden)
    branch = (lax.dot_general(grad_gate, w_gate, CONTRACT_LAST, preferred_element_type=jnp.float32)
              + lax.dot_general(grad_up, w_up, CONTRACT_LAST, preferred_element_type=jnp.float32))
    return (grad_out.astype(jnp.float32) + branch).astype(jnp.bfloat16)


def expert_forward(tokens, w_one, w_three, w_two):
    pre_gate = jnp.einsum('secd,edf->secf', tokens, w_one, preferred_element_type=jnp.float32)
    pre_up = jnp.einsum('secd,edf->secf', tokens, w_three, preferred_element_type=jnp.float32)
    hidden = (jax.nn.silu(pre_gate) * pre_up).astype(jnp.bfloat16)
    return jnp.einsum('secf,efd->secd', hidden, w_two, preferred_element_type=jnp.float32).astype(jnp.bfloat16)


def expert_backward(tokens, grad_rows, gate_rows, w_one, w_three, w_two):
    pre_gate = jnp.einsum('secd,edf->secf', tokens, w_one, preferred_element_type=jnp.float32)
    pre_up = jnp.einsum('secd,edf->secf', tokens, w_three, preferred_element_type=jnp.float32)
    hidden = (jax.nn.silu(pre_gate) * pre_up).astype(jnp.bfloat16)
    out_rows = jnp.einsum('secf,efd->secd', hidden, w_two, preferred_element_type=jnp.float32).astype(jnp.bfloat16)
    grad_mix = jnp.sum(grad_rows.astype(jnp.float32) * out_rows.astype(jnp.float32), axis=-1)
    grad_out = (gate_rows[..., None] * grad_rows).astype(jnp.bfloat16)
    grad_w_two = jnp.einsum('secf,secd->efd', hidden, grad_out, preferred_element_type=jnp.float32)
    grad_hidden = jnp.einsum('secd,efd->secf', grad_out, w_two, preferred_element_type=jnp.float32)
    grad_gate, grad_up = swiglu_grad(pre_gate, pre_up, grad_hidden)
    grad_w_one = jnp.einsum('secd,secf->edf', tokens, grad_gate, preferred_element_type=jnp.float32)
    grad_w_three = jnp.einsum('secd,secf->edf', tokens, grad_up, preferred_element_type=jnp.float32)
    grad_tokens = (jnp.einsum('secf,edf->secd', grad_gate, w_one, preferred_element_type=jnp.float32)
                   + jnp.einsum('secf,edf->secd', grad_up, w_three, preferred_element_type=jnp.float32)).astype(jnp.bfloat16)
    return grad_tokens, grad_mix, grad_w_one, grad_w_three, grad_w_two


def solution(mesh):
    group = mesh.shape['ep']
    tok_spec = P(('dp', 'ep'), None)
    exp_spec = P('ep', None, None)
    full_spec = P(None, None)
    grad_spec = P(('dp', 'ep'), None, None)

    def device_program(x_in, grad_y, ids_a, gate_a, ids_b, gate_b, w1_a, w3_a, w2_a, w1_b, w3_b, w2_b,
                       wg_mid, wu_mid, wd_mid, wg_top, wu_top, wd_top):
        n_tok, hidden_dim = x_in.shape
        top_k = ids_a.shape[1]
        n_local = w1_a.shape[0]
        n_exp = n_local * group
        capacity = 2 * n_tok * top_k // n_exp

        def send_rows(rows, filler):
            picked = jnp.take(rows, filler // top_k, axis=0, mode='fill', fill_value=0)
            return lax.all_to_all(picked.reshape(group, n_local, capacity, hidden_dim), 'ep', 0, 0, tiled=True)

        def send_gates(gate, filler):
            picked = jnp.take(gate.reshape(-1), filler, axis=0, mode='fill', fill_value=0)
            return lax.all_to_all(picked.reshape(group, n_local, capacity), 'ep', 0, 0, tiled=True)

        def return_rows(expert_rows, pair_rows):
            returned = lax.all_to_all(expert_rows, 'ep', 0, 0, tiled=True)
            flat_rows = returned.reshape((n_exp * capacity,) + returned.shape[3:])
            return jnp.take(flat_rows, pair_rows, axis=0).reshape((n_tok, top_k) + returned.shape[3:])

        def combine(x_rows, gate, out_pairs):
            return (x_rows.astype(jnp.float32) + jnp.sum(gate[:, :, None] * out_pairs, axis=1)).astype(jnp.bfloat16)

        def moe_backward(tokens, grad_out, gate, pair_rows, filler, w_one, w_three, w_two):
            grad_rows = send_rows(grad_out, filler)
            gate_rows = send_gates(gate, filler)
            grad_tokens, grad_mix, grad_one, grad_three, grad_two = expert_backward(
                tokens, grad_rows, gate_rows, w_one, w_three, w_two)
            grad_pairs = return_rows(grad_tokens, pair_rows)
            grad_gate = return_rows(grad_mix, pair_rows)
            grad_in = (grad_out.astype(jnp.float32) + jnp.sum(grad_pairs, axis=1, dtype=jnp.float32)).astype(jnp.bfloat16)
            return grad_in, grad_one, grad_three, grad_two, grad_gate

        rows_a, filler_a = route_pairs(ids_a, n_exp, capacity)
        rows_b, filler_b = route_pairs(ids_b, n_exp, capacity)

        tokens_a = send_rows(x_in, filler_a)
        x_a = combine(x_in, gate_a, return_rows(expert_forward(tokens_a, w1_a, w3_a, w2_a), rows_a))
        x_mid = dense_forward(x_a, wg_mid, wu_mid, wd_mid)
        tokens_b = send_rows(x_mid, filler_b)
        x_b = combine(x_mid, gate_b, return_rows(expert_forward(tokens_b, w1_b, w3_b, w2_b), rows_b))
        y_out = dense_forward(x_b, wg_top, wu_top, wd_top)

        grad_b = dense_backward(x_b, grad_y, wg_top, wu_top, wd_top)
        redone_b = send_rows(x_mid, filler_b)
        grad_mid, dw1_b, dw3_b, dw2_b, dgate_b = moe_backward(redone_b, grad_b, gate_b, rows_b, filler_b, w1_b, w3_b, w2_b)
        grad_a = dense_backward(x_a, grad_mid, wg_mid, wu_mid, wd_mid)
        dx_in, dw1_a, dw3_a, dw2_a, dgate_a = moe_backward(tokens_a, grad_a, gate_a, rows_a, filler_a, w1_a, w3_a, w2_a)
        return y_out, dx_in, dw1_a, dw3_a, dw2_a, dw1_b, dw3_b, dw2_b, dgate_a, dgate_b

    in_specs = (tok_spec, tok_spec, tok_spec, tok_spec, tok_spec, tok_spec,
                exp_spec, exp_spec, exp_spec, exp_spec, exp_spec, exp_spec,
                full_spec, full_spec, full_spec, full_spec, full_spec, full_spec)
    out_specs = (tok_spec, tok_spec, grad_spec, grad_spec, grad_spec, grad_spec, grad_spec, grad_spec, tok_spec, tok_spec)
    return jax.shard_map(device_program, mesh=mesh, in_specs=in_specs, out_specs=out_specs, check_vma=False)
```

profile of v0, /device:TPU:0, one launch (start us, length us, event | category | flops | bytes accessed | tf_op | source)
XLA Modules:
  0.0 1865.4 jit_solution(8781886823193482584)
XLA Ops:
  8.2 15.5 scatter_custom_fusion
  24.5 35.7 %gather_fusion = bf16[8192,512]{1,0:T(8,128)(2,1)} fusion(bf16[2048,512]{1,0:T(8,128)(2,1)} %param.26, s32[8192]{0:T(1024)S(1)} %get-tuple-element.61), kind=kCustom, calls=%fused_computation.clone | custom fusion | bytes 16809984 | tf_op jit(solution)/shard_map/jit(_take)/gather | solution.py:85
  64.9 97.9 %all_to_all.61 = bf16[4,2,1024,512]{3,2,1,0:T(8,128)(2,1)} all-to-all(bf16[4,2,1024,512]{3,2,1,0:T(8,128)(2,1)S(1)} %bitcast.254), channel_id=1, replica_groups=mesh['dp'=4,'ep'=4] {'ep'}, dimensions={0} | all-to-all | bytes 16777216 | tf_op jit(solution)/shard_map/all_to_all | solution.py:86
  162.7 28.0 %fusion.40 = f32[2,4,1024,1792]{3,2,1,0:T(8,128)} fusion(bf16[4,2,1024,512]{3,2,1,0:T(8,128)(2,1)} %all_to_all.61, bf16[2,512,1792]{2,1,0:T(8,128)(2,1)} %param.32), kind=kOutput, calls=%fused_computation.88 | convolution fusion | flops 15032385536 | bytes 70778880 | tf_op jit(solution)/shard_map/secd,edf->secf/dot_general | solution.py:46
  190.7 54.7 %fusion.15 = (bf16[4,2,1024,1792]{3,2,0,1:T(8,128)(2,1)}, f32[2,4,1024,1792]{3,2,1,0:T(8,128)}) fusion(f32[2,4,1024,1792]{3,2,1,0:T(8,128)} %fusion.40, bf16[2,512,1792]{2,1,0:T(8,128)(2,1)} %param.33, bf16[4,2,1024,512]{3,2,1,0:T(8,128)(2,1)} %all_to_all.61), kind=kOutput, calls=%fused_computation.38 | convolution fusion | flops 15120465920 | bytes 158859264 | tf_op jit(solution)/shard_map/secd,edf->secf/dot_general | solution.py:47
  245.4 21.6 %convert_bitcast_fusion.1 = bf16[4,2,1024,512]{2,3,0,1:T(8,128)(2,1)} fusion(bf16[4,2,1024,1792]{3,2,0,1:T(8,128)(2,1)} %get-tuple-element.62, bf16[2,1792,512]{2,1,0:T(8,128)(2,1)} %param.34), kind=kOutput, calls=%fused_computation.77 | convolution fusion | flops 15036579840 | bytes 41418752 | tf_op jit(solution)/shard_map/secf,efd->secd/dot_general | solution.py:49
  287.3 15.5 scatter_custom_fusion.1
  303.6 70.1 %all-to-all-done.1 = bf16[4,2,1024,512]{2,3,1,0:T(8,128)(2,1)} async-done(((bf16[4,2,1024,512]{2,3,1,0:T(8,128)(2,1)}), bf16[4,2,1024,512]{2,3,1,0:T(8,128)(2,1)}, u32[]{:S(2)}, u32[]{:S(2)}) %all-to-all-start.1) | async-done | bytes 8388640 | tf_op jit(solution)/shard_map/all_to_all | solution.py:93
  385.1 21.9 %gather_fusion.1 = bf16[4096,512]{1,0:T(8,128)(2,1)} fusion(bf16[8192,512]{1,0:T(8,128)(2,1)} %bitcast.250, s32[4096]{0:T(1024)S(1)} %broadcast_clamp_fusion.3), kind=kCustom, calls=%fused_computation.1.clone | custom fusion | bytes 8404992 | tf_op jit(solution)/shard_map/jit(_take)/gather | solution.py:95
  422.9 14.1 multiply_reduce_fusion.1
  452.3 12.9 add_convert_fusion.8
  465.2 35.7 %gather_fusion.2 = bf16[8192,512]{1,0:T(8,128)(2,1)} fusion(bf16[2048,512]{1,0:T(8,128)(2,1)} %add_convert_fusion.8, s32[8192]{0:T(1024)S(1)} %get-tuple-element.59), kind=kCustom, calls=%fused_computation.4.clone | custom fusion | bytes 16809984 | tf_op jit(solution)/shard_map/jit(_take)/gather | solution.py:85
  505.5 97.0 %all_to_all.62 = bf16[4,2,1024,512]{3,2,1,0:T(8,128)(2,1)} all-to-all(bf16[4,2,1024,512]{3,2,1,0:T(8,128)(2,1)S(1)} %bitcast.255), channel_id=1, replica_groups=mesh['dp'=4,'ep'=4] {'ep'}, dimensions={0} | all-to-all | bytes 16777216 | tf_op jit(solution)/shard_map/all_to_all | solution.py:86
  602.5 28.0 %fusion.36 = f32[2,4,1024,1792]{3,2,1,0:T(8,128)} fusion(bf16[4,2,1024,512]{3,2,1,0:T(8,128)(2,1)} %all_to_all.62, bf16[2,512,1792]{2,1,0:T(8,128)(2,1)} %param.35), kind=kOutput, calls=%fused_computation.84 | convolution fusion | flops 15032385536 | bytes 70778880 | tf_op jit(solution)/shard_map/secd,edf->secf/dot_general | solution.py:46
  630.5 54.8 %fusion.10 = (bf16[4,2,1024,1792]{3,2,0,1:T(8,128)(2,1)}, f32[2,4,1024,1792]{3,2,1,0:T(8,128)}) fusion(f32[2,4,1024,1792]{3,2,1,0:T(8,128)} %fusion.36, bf16[2,512,1792]{2,1,0:T(8,128)(2,1)} %param.36, bf16[4,2,1024,512]{3,2,1,0:T(8,128)(2,1)} %all_to_all.62), kind=kOutput, calls=%fused_computation.29 | convolution fusion | flops 15120465920 | bytes 158859264 | tf_op jit(solution)/shard_map/secd,edf->secf/dot_general | solution.py:47
  685.3 21.6 %convert_bitcast_fusion = bf16[4,2,1024,512]{2,3,0,1:T(8,128)(2,1)} fusion(bf16[4,2,1024,1792]{3,2,0,1:T(8,128)(2,1)} %get-tuple-element.64, bf16[2,1792,512]{2,1,0:T(8,128)(2,1)} %param.37), kind=kOutput, calls=%fused_computation.75 | convolution fusion | flops 15036579840 | bytes 41418752 | tf_op jit(solution)/shard_map/secf,efd->secd/dot_general | solution.py:49
  721.6 45.5 %gather_fusion.4 = f32[8192]{0:T(1024)S(1)} fusion(f32[4096]{0:T(1024)S(1)} %reshape.203, s32[8192]{0:T(1024)S(1)} %copy-done.31), kind=kCustom, calls=%fused_computation.2.clone | custom fusion | bytes 98304 | tf_op jit(solution)/shard_map/jit(_take)/gather | solution.py:89
  779.1 34.4 %all-to-all-done.3 = bf16[4,2,1024,512]{2,3,1,0:T(8,128)(2,1)} async-done(((bf16[4,2,1024,512]{2,3,1,0:T(8,128)(2,1)}), bf16[4,2,1024,512]{2,3,1,0:T(8,128)(2,1)}, u32[]{:S(2)}, u32[]{:S(2)}) %all-to-all-start.3) | async-done | bytes 8388640 | tf_op jit(solution)/shard_map/all_to_all | solution.py:93
  828.8 21.9 %gather_fusion.3 = bf16[4096,512]{1,0:T(8,128)(2,1)} fusion(bf16[8192,512]{1,0:T(8,128)(2,1)} %bitcast.251, s32[4096]{0:T(1024)S(1)} %broadcast_clamp_fusion.2), kind=kCustom, calls=%fused_computation.7.clone | custom fusion | bytes 8404992 | tf_op jit(solution)/shard_map/jit(_take)/gather | solution.py:95
  866.5 14.1 multiply_reduce_fusion
  907.6 18.2 add_convert_fusion.5
  925.8 35.6 %gather_fusion.5 = bf16[8192,512]{1,0:T(8,128)(2,1)} fusion(bf16[2048,512]{1,0:T(8,128)(2,1)} %add_convert_fusion.5, s32[8192]{0:T(1024)S(1)} %copy-done.16), kind=kCustom, calls=%fused_computation.5.clone | custom fusion | bytes 16809984 | tf_op jit(solution)/shard_map/jit(_take)/gather | solution.py:85
  986.7 45.5 %gather_fusion.7 = f32[8192]{0:T(1024)S(1)} fusion(f32[4096]{0:T(1024)S(1)} %reshape.207, s32[8192]{0:T(1024)S(1)} %copy-done.30), kind=kCustom, calls=%fused_computation.10.clone | custom fusion | bytes 98304 | tf_op jit(solution)/shard_map/jit(_take)/gather | solution.py:89
  1033.7 45.3 %all-to-all-done.5 = bf16[4,2,1024,512]{2,3,1,0:T(8,128)(2,1)} async-done(((bf16[4,2,1024,512]{2,3,1,0:T(8,128)(2,1)}), bf16[4,2,1024,512]{2,3,1,0:T(8,128)(2,1)}, u32[]{:S(2)}, u32[]{:S(2)}) %all-to-all-start.5) | async-done | bytes 8388640 | tf_op jit(solution)/shard_map/all_to_all | solution.py:86
  1082.9 64.1 %fusion.9 = (bf16[4,2,1024,1792]{3,2,0,1:T(8,128)(2,1)}, bf16[4,2,1024,1792]{3,2,0,1:T(8,128)(2,1)}) fusion(f32[2,4,1024,1792]{3,2,1,0:T(8,128)} %fusion.36, f32[2,4,1024,1792]{3,2,1,0:T(8,128)} %get-tuple-element.65, bf16[2,1792,512]{2,1,0:T(8,128)(2,1)} %param.37, f32[4,2,1024]{2,0,1:T(4,128)S(1)} %copy.181, bf16[4,2,1024,512]{2,3,1,0:T(8,128)(2,1)} %all-to-all-done.5), kind=kOutput, calls=%fused_computation.27 | convolution fusion | flops 15235809280 | bytes 188252160 | tf_op jit(solution)/shard_map/secd,efd->secf/dot_general | solution.py:60
  1147.0 25.1 %fusion.85 = f32[2,4,1024,512]{3,2,1,0:T(8,128)} fusion(bf16[4,2,1024,1792]{3,2,0,1:T(8,128)(2,1)} %get-tuple-element.57, bf16[2,512,1792]{2,1,0:T(8,128)(2,1)} %param.35), kind=kOutput, calls=%fused_computation.129 | convolution fusion | flops 15032385536 | bytes 49807360 | tf_op jit(solution)/shard_map/secf,edf->secd/dot_general | solution.py:64
  1172.2 25.5 %fusion.32 = bf16[4,2,1024,512]{3,2,0,1:T(8,128)(2,1)} fusion(f32[2,4,1024,512]{3,2,1,0:T(8,128)} %fusion.85, bf16[4,2,1024,1792]{3,2,0,1:T(8,128)(2,1)} %get-tuple-element.56, bf16[2,512,1792]{2,1,0:T(8,128)(2,1)} %param.36), kind=kOutput, calls=%fused_computation.72 | convolution fusion | flops 15040774144 | bytes 58195968 | tf_op jit(solution)/shard_map/secf,edf->secd/dot_general | solution.py:65
  1211.9 13.4 add_convert_fusion.6
  1235.8 67.5 %all-to-all-done.6 = bf16[4,2,1024,512]{3,2,1,0:T(8,128)(2,1)} async-done(((bf16[4,2,1024,512]{3,2,1,0:T(8,128)(2,1)}), bf16[4,2,1024,512]{3,2,1,0:T(8,128)(2,1)}, u32[]{:S(2)}, u32[]{:S(2)}) %all-to-all-start.6) | async-done | bytes 8388640 | tf_op jit(solution)/shard_map/all_to_all | solution.py:93
  1307.4 21.9 %gather_fusion.6 = bf16[4096,512]{1,0:T(8,128)(2,1)} fusion(bf16[8192,512]{1,0:T(8,128)(2,1)} %bitcast.33, s32[4096]{0:T(1024)S(1)} %copy-done.28), kind=kCustom, calls=%fused_computation.8.clone | custom fusion | bytes 8404992 | tf_op jit(solution)/shard_map/jit(_take)/gather | solution.py:95
  1345.1 15.7 reduce_sum.82
  1371.5 13.7 fusion.45
  1385.2 19.6 %add_convert_fusion.3 = bf16[2048,512]{1,0:T(8,128)(2,1)} fusion(f32[2048,512]{1,0:T(8,128)} %fusion.45, bf16[512,1792]{1,0:T(8,128)(2,1)} %param.38, f32[2048,1792]{1,0:T(8,128)} %fusion.113, f32[2048,1792]{1,0:T(8,128)} %fusion.112, f32[2048,1792]{1,0:T(8,128)} %fusion.114, f32[2048,512]{1,0:T(8,128)S(1)} %copy-done.7, bf16[2048,512]{1,0:T(8,128)(2,1)S(1)} %copy-done.4), kind=kOutput, calls=%fused_computation.111 | convolution fusion | flops 3802136576 | bytes 58458112 | tf_op jit(solution)/shard_map/dot_general | solution.py:40
  1404.8 35.6 %gather_fusion.8 = bf16[8192,512]{1,0:T(8,128)(2,1)} fusion(bf16[2048,512]{1,0:T(8,128)(2,1)} %add_convert_fusion.3, s32[8192]{0:T(1024)S(1)} %copy-done.14), kind=kCustom, calls=%fused_computation.6.clone | custom fusion | bytes 16809984 | tf_op jit(solution)/shard_map/jit(_take)/gather | solution.py:85
  1447.9 11.7 copy.188
  1465.2 23.0 %fusion.71 = f32[2,512,1792]{2,1,0:T(8,128)} fusion(bf16[4,2,1024,512]{3,2,1,0:T(8,128)(2,1)} %all_to_all.62, bf16[4,2,1024,1792]{3,2,0,1:T(8,128)(2,1)} %get-tuple-element.56), kind=kOutput, calls=%fused_computation.105 | convolution fusion | flops 15032385536 | bytes 45088768 | tf_op jit(solution)/shard_map/secd,secf->edf/dot_general | solution.py:63
  1488.2 23.0 %fusion.68 = f32[2,512,1792]{2,1,0:T(8,128)} fusion(bf16[4,2,1024,512]{3,2,1,0:T(8,128)(2,1)} %all_to_all.62, bf16[4,2,1024,1792]{3,2,0,1:T(8,128)(2,1)} %get-tuple-element.57), kind=kOutput, calls=%fused_computation.104 | convolution fusion | flops 15032385536 | bytes 45088768 | tf_op jit(solution)/shard_map/secd,secf->edf/dot_general | solution.py:62
  1511.2 28.1 %fusion.56 = f32[2,1792,512]{2,1,0:T(8,128)} fusion(bf16[4,2,1024,1792]{3,2,0,1:T(8,128)(2,1)} %get-tuple-element.64, f32[4,2,1024]{2,0,1:T(4,128)S(1)} %copy-done.44, bf16[4,2,1024,512]{2,3,1,0:T(8,128)(2,1)} %all-to-all-done.5), kind=kOutput, calls=%fused_computation.100 | convolution fusion | flops 15044968448 | bytes 45121536 | tf_op jit(solution)/shard_map/secf,secd->efd/dot_general | solution.py:59
  1540.1 23.0 %gather_fusion.11 = f32[4096]{0:T(1024)S(1)} fusion(f32[8192]{0:T(1024)S(1)} %bitcast.248, s32[4096]{0:T(1024)S(1)} %copy-done.29), kind=kCustom, calls=%fused_computation.11.clone | custom fusion | bytes 49152 | tf_op jit(solution)/shard_map/jit(_take)/gather | solution.py:95
  1579.7 64.1 %fusion.4 = (bf16[4,2,1024,1792]{3,2,0,1:T(8,128)(2,1)}, bf16[4,2,1024,1792]{3,2,0,1:T(8,128)(2,1)}) fusion(f32[2,4,1024,1792]{3,2,1,0:T(8,128)} %fusion.40, f32[2,4,1024,1792]{3,2,1,0:T(8,128)} %get-tuple-element.63, bf16[2,1792,512]{2,1,0:T(8,128)(2,1)} %param.34, f32[4,2,1024]{2,0,1:T(4,128)S(1)} %copy-done.42, bf16[4,2,1024,512]{2,3,1,0:T(8,128)(2,1)} %all-to-all-done.8), kind=kOutput, calls=%fused_computation.20 | convolution fusion | flops 15235809280 | bytes 188252160 | tf_op jit(solution)/shard_map/secd,efd->secf/dot_general | solution.py:60
  1643.8 25.2 %fusion.80 = f32[2,4,1024,512]{3,2,1,0:T(8,128)} fusion(bf16[4,2,1024,1792]{3,2,0,1:T(8,128)(2,1)} %get-tuple-element.55, bf16[2,512,1792]{2,1,0:T(8,128)(2,1)} %param.32), kind=kOutput, calls=%fused_computation.124 | convolution fusion | flops 15032385536 | bytes 49807360 | tf_op jit(solution)/shard_map/secf,edf->secd/dot_general | solution.py:64
  1669.0 25.3 %fusion.33 = bf16[4,2,1024,512]{3,2,0,1:T(8,128)(2,1)} fusion(f32[2,4,1024,512]{3,2,1,0:T(8,128)} %fusion.80, bf16[4,2,1024,1792]{3,2,0,1:T(8,128)(2,1)} %get-tuple-element.54, bf16[2,512,1792]{2,1,0:T(8,128)(2,1)} %param.33), kind=kOutput, calls=%fused_computation.73 | convolution fusion | flops 15040774144 | bytes 58195968 | tf_op jit(solution)/shard_map/secf,edf->secd/dot_general | solution.py:65
  1707.1 23.0 %fusion.65 = f32[2,512,1792]{2,1,0:T(8,128)} fusion(bf16[4,2,1024,512]{3,2,1,0:T(8,128)(2,1)} %all_to_all.61, bf16[4,2,1024,1792]{3,2,0,1:T(8,128)(2,1)} %get-tuple-element.54), kind=kOutput, calls=%fused_computation.103 | convolution fusion | flops 15032385536 | bytes 45088768 | tf_op jit(solution)/shard_map/secd,secf->edf/dot_general | solution.py:63
  1730.1 23.0 %fusion.62 = f32[2,512,1792]{2,1,0:T(8,128)} fusion(bf16[4,2,1024,512]{3,2,1,0:T(8,128)(2,1)} %all_to_all.61, bf16[4,2,1024,1792]{3,2,0,1:T(8,128)(2,1)} %get-tuple-element.55), kind=kOutput, calls=%fused_computation.102 | convolution fusion | flops 15032385536 | bytes 45088768 | tf_op jit(solution)/shard_map/secd,secf->edf/dot_general | solution.py:62
  1753.1 27.9 %fusion.59 = f32[2,1792,512]{2,1,0:T(8,128)} fusion(bf16[4,2,1024,1792]{3,2,0,1:T(8,128)(2,1)} %get-tuple-element.62, f32[4,2,1024]{2,0,1:T(4,128)S(1)} %copy-done.42, bf16[4,2,1024,512]{2,3,1,0:T(8,128)(2,1)} %all-to-all-done.8), kind=kOutput, calls=%fused_computation.101 | convolution fusion | flops 15044968448 | bytes 45121536 | tf_op jit(solution)/shard_map/secf,secd->efd/dot_general | solution.py:59
  1781.8 23.0 %gather_fusion.10 = f32[4096]{0:T(1024)S(1)} fusion(f32[8192]{0:T(1024)S(1)} %bitcast.249, s32[4096]{0:T(1024)S(1)} %copy-done.26), kind=kCustom, calls=%fused_computation.3.clone | custom fusion | bytes 49152 | tf_op jit(solution)/shard_map/jit(_take)/gather | solution.py:95
  1806.8 21.9 %gather_fusion.9 = bf16[4096,512]{1,0:T(8,128)(2,1)} fusion(bf16[8192,512]{1,0:T(8,128)(2,1)} %bitcast.41, s32[4096]{0:T(1024)S(1)} %copy-done.26), kind=kCustom, calls=%fused_computation.9.clone | custom fusion | bytes 8404992 | tf_op jit(solution)/shard_map/jit(_take)/gather | solution.py:95
  1844.6 15.5 reduce_sum.83
  (213 shorter events, 318.1 us)
Async XLA Ops:
  0.6 888.0 %copy-start = (bf16[512,1792]{1,0:T(8,128)(2,1)S(1)}, bf16[512,1792]{1,0:T(8,128)(2,1)}, u32[]{:S(2)}) copy-start(bf16[512,1792]{1,0:T(8,128)(2,1)} %param.42) | copy-start | bytes 5505028
  3.1 57.1 %copy-start.19 = (s32[4096]{0:T(1024)}, s32[4096]{0:T(1024)S(1)}, u32[]{:S(2)}) copy-start(s32[4096]{0:T(1024)S(1)} %eq.50) | copy-start | bytes 49156
  23.8 36.4 %copy-start.9 = (s32[8192]{0:T(1024)}, s32[8192]{0:T(1024)S(1)}, u32[]{:S(2)}) copy-start(s32[8192]{0:T(1024)S(1)} %scatter_custom_fusion) | copy-start | bytes 98308
  23.8 36.3 %copy-start.32 = (pred[8192]{0:T(1024)(128)(4,1)}, pred[8192]{0:T(1024)(128)(4,1)S(1)}, u32[]{:S(2)}) copy-start(pred[8192]{0:T(1024)(128)(4,1)S(1)} %compare_and_fusion.1) | copy-start | bytes 24580
  24.5 35.7 %copy-start.13 = (s32[8192]{0:T(1024)}, s32[8192]{0:T(1024)S(1)}, u32[]{:S(2)}) copy-start(s32[8192]{0:T(1024)S(1)} %get-tuple-element.61) | copy-start | bytes 98308
  274.6 28.2 %copy-start.20 = (s32[4096]{0:T(1024)S(1)}, s32[4096]{0:T(1024)}, u32[]{:S(2)}) copy-start(s32[4096]{0:T(1024)} %copy-done.19) | copy-start | bytes 49156
  274.6 28.2 %copy-start.24 = (s32[4096]{0:T(1024)S(1)}, s32[4096]{0:T(1024)}, u32[]{:S(2)}) copy-start(s32[4096]{0:T(1024)} %copy-done.23) | copy-start | bytes 49156
  274.6 99.0 %all-to-all-start.1 = ((bf16[4,2,1024,512]{2,3,1,0:T(8,128)(2,1)}), bf16[4,2,1024,512]{2,3,1,0:T(8,128)(2,1)}, u32[]{:S(2)}, u32[]{:S(2)}) async-start(bf16[4,2,1024,512]{2,3,1,0:T(8,128)(2,1)} %copy.169), calls=%async_computation.1 | async-start | bytes 16777216 | tf_op jit(solution)/shard_map/all_to_all | solution.py:93
  281.7 103.4 %copy-start.17 = (s32[4096]{0:T(1024)}, s32[4096]{0:T(1024)S(1)}, u32[]{:S(2)}) copy-start(s32[4096]{0:T(1024)S(1)} %eq.58) | copy-start | bytes 49156
  283.6 139.3 %copy-start.5 = (f32[2048,2]{1,0:T(8,128)}, f32[2048,2]{1,0:T(8,128)S(1)}, u32[]{:S(2)}) copy-start(f32[2048,2]{1,0:T(8,128)S(1)} %copy.162) | copy-start | bytes 49156
  302.8 82.3 %copy-start.11 = (s32[8192]{0:T(1024)}, s32[8192]{0:T(1024)S(1)}, u32[]{:S(2)}) copy-start(s32[8192]{0:T(1024)S(1)} %scatter_custom_fusion.1) | copy-start | bytes 98308
  302.9 104.2 %copy-start.36 = (pred[4096]{0:T(1024)(128)(4,1)}, pred[4096]{0:T(1024)(128)(4,1)S(1)}, u32[]{:S(2)}) copy-start(pred[4096]{0:T(1024)(128)(4,1)S(1)} %compare_and_fusion.3) | copy-start | bytes 12292
  302.9 197.9 %copy-start.34 = (pred[8192]{0:T(1024)(128)(4,1)}, pred[8192]{0:T(1024)(128)(4,1)S(1)}, u32[]{:S(2)}) copy-start(pred[8192]{0:T(1024)(128)(4,1)S(1)} %compare_and_fusion) | copy-start | bytes 24580
  302.9 82.2 %copy-start.25 = (s32[4096]{0:T(1024)}, s32[4096]{0:T(1024)S(1)}, u32[]{:S(2)}) copy-start(s32[4096]{0:T(1024)S(1)} %broadcast_clamp_fusion.3) | copy-start | bytes 49156
  303.6 161.6 %copy-start.15 = (s32[8192]{0:T(1024)}, s32[8192]{0:T(1024)S(1)}, u32[]{:S(2)}) copy-start(s32[8192]{0:T(1024)S(1)} %get-tuple-element.59) | copy-start | bytes 98308
  422.9 14.1 copy-start.2
  422.9 14.9 copy-start.54
  714.5 99.0 %all-to-all-start.3 = ((bf16[4,2,1024,512]{2,3,1,0:T(8,128)(2,1)}), bf16[4,2,1024,512]{2,3,1,0:T(8,128)(2,1)}, u32[]{:S(2)}, u32[]{:S(2)}) async-start(bf16[4,2,1024,512]{2,3,1,0:T(8,128)(2,1)} %copy.178), calls=%async_computation.3 | async-start | bytes 16777216 | tf_op jit(solution)/shard_map/all_to_all | solution.py:93
  721.5 45.6 %copy-start.12 = (s32[8192]{0:T(1024)S(1)}, s32[8192]{0:T(1024)}, u32[]{:S(2)}) copy-start(s32[8192]{0:T(1024)} %copy-done.11) | copy-start | bytes 98308
  721.5 46.2 %copy-start.18 = (s32[4096]{0:T(1024)S(1)}, s32[4096]{0:T(1024)}, u32[]{:S(2)}) copy-start(s32[4096]{0:T(1024)} %copy-done.17) | copy-start | bytes 49156
  721.5 46.2 %copy-start.22 = (s32[4096]{0:T(1024)S(1)}, s32[4096]{0:T(1024)}, u32[]{:S(2)}) copy-start(s32[4096]{0:T(1024)} %copy-done.21) | copy-start | bytes 49156
  767.8 82.9 %copy-start.38 = (pred[4096]{0:T(1024)(128)(4,1)}, pred[4096]{0:T(1024)(128)(4,1)S(1)}, u32[]{:S(2)}) copy-start(pred[4096]{0:T(1024)(128)(4,1)S(1)} %compare_and_fusion.2) | copy-start | bytes 12292
  767.8 61.0 %copy-start.27 = (s32[4096]{0:T(1024)}, s32[4096]{0:T(1024)S(1)}, u32[]{:S(2)}) copy-start(s32[4096]{0:T(1024)S(1)} %broadcast_clamp_fusion.2) | copy-start | bytes 49156
  813.5 166.9 %all-to-all-start.4 = ((f32[4,2,1024]{2,1,0:T(2,128)}), f32[4,2,1024]{2,1,0:T(2,128)}, u32[]{:S(2)}, u32[]{:S(2)}) async-start(f32[4,2,1024]{2,1,0:T(2,128)} %reshape.204), calls=%async_computation.4 | async-start | bytes 65536 | tf_op jit(solution)/shard_map/all_to_all | solution.py:90
  866.5 14.9 copy-start.48
  907.6 18.2 copy-start.16
  925.8 35.6 %copy-start.35 = (pred[8192]{0:T(1024)(128)(4,1)S(1)}, pred[8192]{0:T(1024)(128)(4,1)}, u32[]{:S(2)}) copy-start(pred[8192]{0:T(1024)(128)(4,1)} %copy-done.34) | copy-start | bytes 24580
  980.4 98.6 %all-to-all-start.5 = ((bf16[4,2,1024,512]{2,3,1,0:T(8,128)(2,1)}), bf16[4,2,1024,512]{2,3,1,0:T(8,128)(2,1)}, u32[]{:S(2)}, u32[]{:S(2)}) async-start(bf16[4,2,1024,512]{2,3,1,0:T(8,128)(2,1)} %copy.182), calls=%async_computation.5 | async-start | bytes 16777216 | tf_op jit(solution)/shard_map/all_to_all | solution.py:86
  986.7 45.6 %copy-start.10 = (s32[8192]{0:T(1024)S(1)}, s32[8192]{0:T(1024)}, u32[]{:S(2)}) copy-start(s32[8192]{0:T(1024)} %copy-done.9) | copy-start | bytes 98308
  1033.7 113.4 %copy-start.43 = (f32[4,2,1024]{2,0,1:T(4,128)}, f32[4,2,1024]{2,0,1:T(4,128)S(1)}, u32[]{:S(2)}) copy-start(f32[4,2,1024]{2,0,1:T(4,128)S(1)} %copy.181) | copy-start | bytes 98308
  1079.0 125.7 %all-to-all-start.7 = ((f32[4,2,1024]{2,1,0:T(2,128)}), f32[4,2,1024]{2,1,0:T(2,128)}, u32[]{:S(2)}, u32[]{:S(2)}) async-start(f32[4,2,1024]{2,1,0:T(2,128)} %reshape.208), calls=%async_computation.7 | async-start | bytes 65536 | tf_op jit(solution)/shard_map/all_to_all | solution.py:90
  1204.8 98.6 %all-to-all-start.6 = ((bf16[4,2,1024,512]{3,2,1,0:T(8,128)(2,1)}), bf16[4,2,1024,512]{3,2,1,0:T(8,128)(2,1)}, u32[]{:S(2)}, u32[]{:S(2)}) async-start(bf16[4,2,1024,512]{3,2,1,0:T(8,128)(2,1)} %copy.185), calls=%async_computation.6 | async-start | bytes 16777216 | tf_op jit(solution)/shard_map/all_to_all | solution.py:93
  1225.3 82.1 %copy-start.28 = (s32[4096]{0:T(1024)S(1)}, s32[4096]{0:T(1024)}, u32[]{:S(2)}) copy-start(s32[4096]{0:T(1024)} %copy-done.27) | copy-start | bytes 49156
  1303.3 156.3 %all-to-all-start.11 = ((f32[4,2,1024]{2,1,0:T(2,128)}), f32[4,2,1024]{2,1,0:T(2,128)}, u32[]{:S(2)}, u32[]{:S(2)}) async-start(f32[4,2,1024]{2,1,0:T(2,128)} %copy.205), calls=%async_computation.11 | async-start | bytes 65536 | tf_op jit(solution)/shard_map/all_to_all | solution.py:93
  1307.4 21.9 %copy-start.39 = (pred[4096]{0:T(1024)(128)(4,1)S(1)}, pred[4096]{0:T(1024)(128)(4,1)}, u32[]{:S(2)}) copy-start(pred[4096]{0:T(1024)(128)(4,1)} %copy-done.38) | copy-start | bytes 12292
  1345.1 15.7 copy-start.51
  1385.2 19.6 %copy-start.14 = (s32[8192]{0:T(1024)S(1)}, s32[8192]{0:T(1024)}, u32[]{:S(2)}) copy-start(s32[8192]{0:T(1024)} %copy-done.13) | copy-start | bytes 98308
  1404.8 35.6 %copy-start.33 = (pred[8192]{0:T(1024)(128)(4,1)S(1)}, pred[8192]{0:T(1024)(128)(4,1)}, u32[]{:S(2)}) copy-start(pred[8192]{0:T(1024)(128)(4,1)} %copy-done.32) | copy-start | bytes 24580
  1459.6 105.5 %all-to-all-start.8 = ((bf16[4,2,1024,512]{2,3,1,0:T(8,128)(2,1)}), bf16[4,2,1024,512]{2,3,1,0:T(8,128)(2,1)}, u32[]{:S(2)}, u32[]{:S(2)}) async-start(bf16[4,2,1024,512]{2,3,1,0:T(8,128)(2,1)} %copy.188), calls=%async_computation.8 | async-start | bytes 16777216 | tf_op jit(solution)/shard_map/all_to_all | solution.py:86
  1488.2 23.0 %copy-start.44 = (f32[4,2,1024]{2,0,1:T(4,128)S(1)}, f32[4,2,1024]{2,0,1:T(4,128)}, u32[]{:S(2)}) copy-start(f32[4,2,1024]{2,0,1:T(4,128)} %copy-done.43) | copy-start | bytes 98308
  1511.2 28.8 %copy-start.29 = (s32[4096]{0:T(1024)S(1)}, s32[4096]{0:T(1024)}, u32[]{:S(2)}) copy-start(s32[4096]{0:T(1024)} %copy-done.27) | copy-start | bytes 49156
  1540.1 23.0 %copy-start.40 = (pred[4096]{0:T(1024)(128)(4,1)S(1)}, pred[4096]{0:T(1024)(128)(4,1)}, u32[]{:S(2)}) copy-start(pred[4096]{0:T(1024)(128)(4,1)} %copy-done.38) | copy-start | bytes 12292
  1565.1 14.6 copy-start.42
  1575.6 125.8 %all-to-all-start.10 = ((f32[4,2,1024]{2,1,0:T(2,128)}), f32[4,2,1024]{2,1,0:T(2,128)}, u32[]{:S(2)}, u32[]{:S(2)}) async-start(f32[4,2,1024]{2,1,0:T(2,128)} %copy.204), calls=%async_computation.10 | async-start | bytes 65536 | tf_op jit(solution)/shard_map/all_to_all | solution.py:93
  1701.4 105.4 %all-to-all-start.9 = ((bf16[4,2,1024,512]{3,2,1,0:T(8,128)(2,1)}), bf16[4,2,1024,512]{3,2,1,0:T(8,128)(2,1)}, u32[]{:S(2)}, u32[]{:S(2)}) async-start(bf16[4,2,1024,512]{3,2,1,0:T(8,128)(2,1)} %copy.191), calls=%async_computation.9 | async-start | bytes 16777216 | tf_op jit(solution)/shard_map/all_to_all | solution.py:93
  1753.1 28.7 %copy-start.26 = (s32[4096]{0:T(1024)S(1)}, s32[4096]{0:T(1024)}, u32[]{:S(2)}) copy-start(s32[4096]{0:T(1024)} %copy-done.25) | copy-start | bytes 49156
  1781.8 23.0 %copy-start.37 = (pred[4096]{0:T(1024)(128)(4,1)S(1)}, pred[4096]{0:T(1024)(128)(4,1)}, u32[]{:S(2)}) copy-start(pred[4096]{0:T(1024)(128)(4,1)} %copy-done.36) | copy-start | bytes 12292
  1833.9 31.1 %copy-start.1 = (bf16[512,1792]{1,0:T(8,128)(2,1)S(1)}, bf16[512,1792]{1,0:T(8,128)(2,1)}, u32[]{:S(2)}) copy-start(bf16[512,1792]{1,0:T(8,128)(2,1)} %param.42) | copy-start | bytes 5505028
  (17 other events, 134.2 us)
where the time goes:
time: 1870 us
  matrix products  726 us (39%)
  local copies, waits for them, and re-layouts  535 us (29%)
  waiting for transfers between devices  217 us (12%)
  blocking collectives  195 us (10%)
  other arithmetic  139 us (7%)
  starting transfers between devices  51 us (3%)
    all_to_all x2, blocking collectives, send_rows(): lax.all_to_all(picked.reshape(group, n_local, capacity, hidden_dim), 'ep'...  195 us
    all_to_all x6, waiting for transfers between devices, return_rows(): returned = lax.all_to_all(expert_rows, 'ep', 0, 0, tiled=True)  172 us
    gather x4, local copies, waits for them, and re-layouts, send_rows(): picked = jnp.take(rows, filler // top_k, axis=0, mode='fill', fill_value=0)  143 us
    gather x6, local copies, waits for them, and re-layouts, return_rows(): jnp.take(flat_rows, pair_rows, axis=0)  134 us
    dot_general x2, matrix products, expert_backward(): jnp.einsum('secd,efd->secf', grad_out, w_two, preferred_element_type=jnp....  128 us
    dot_general x2, matrix products, expert_forward(): jnp.einsum('secd,edf->secf', tokens, w_three, preferred_element_type=jnp....  110 us
    gather x2, local copies, waits for them, and re-layouts, send_gates(): jnp.take(gate.reshape(-1), filler, axis=0, mode='fill', fill_value=0)  91.1 us
    dot_general x2, matrix products, expert_backward(): jnp.einsum('secf,secd->efd', hidden, grad_out, preferred_element_type=jnp...  56 us
  transfers between devices with their start and end apart: 10, of which 4 were waited for; matrix products, arithmetic and copies ran while one was open for 49% of the time, Pallas kernels for 0%

commit v1 on v0

v1 whole, which is shorter than its diff:
```python
import functools

import jax
import jax.numpy as jnp
from jax import lax
from jax.experimental import pallas as pl
from jax.experimental.pallas import tpu as pltpu
from jax.sharding import PartitionSpec as P


F32 = jnp.float32
BF16 = jnp.bfloat16
SUB = 128
WIN = SUB + 16
ROWS = 256
TOK = 256
CHUNK = 256
PACK = 1024
VMEM_LIMIT = 62 * 1024 * 1024

MM = (((1,), (0,)), ((), ()))
LAST = (((1,), (1,)), ((), ()))
FIRST = (((0,), (0,)), ((), ()))


def dot(left, right, dims=MM):
    return lax.dot_general(left, right, dims, preferred_element_type=F32)


def params():
    return pltpu.CompilerParams(dimension_semantics=("arbitrary",), vmem_limit_bytes=VMEM_LIMIT)


def cost(flops, bytes_accessed):
    return pl.CostEstimate(flops=flops, bytes_accessed=bytes_accessed, transcendentals=0)


def route(ids, gate, experts):
    first = ids[..., None, :, 0] == experts[:, None]
    second = ids[..., None, :, 1] == experts[:, None]
    hit = (first | second).astype(jnp.int32)
    ends = jnp.cumsum(hit, axis=-1)
    before = ends - hit
    slots = jnp.where(hit > 0, before, -1)
    gates = jnp.where(first, gate[..., None, :, 0], 0.0) + jnp.where(second, gate[..., None, :, 1], 0.0)
    return slots, gates, before[..., ::SUB], ends[..., -1]


def combine_rows(index, local, win_ref, slots_ref, gates_ref, backs, capacity):
    n_local = len(backs)
    n_exp = slots_ref.shape[1]
    column = lax.broadcasted_iota(jnp.int32, (SUB, WIN), 1)
    tokens = pl.ds(local * SUB, SUB)
    slots = slots_ref[tokens, :]
    gates = None if gates_ref is None else gates_ref[tokens, :]
    total = None
    for exp in range(n_exp):
        start = win_ref[index * n_exp + exp]
        where = slots[:, exp:exp + 1] - start
        pick = jnp.where(column == where, 1.0, 0.0).astype(BF16)
        source = pl.ds(pl.multiple_of(exp // n_local * capacity + start, 16), WIN)
        term = dot(pick, backs[exp % n_local][source, :])
        if gates is not None:
            term = term * gates[:, exp:exp + 1]
        total = term if total is None else total + term
    return total


def zero_all(refs):
    for ref in refs:
        ref[...] = jnp.zeros(ref.shape, ref.dtype)


def swiglu_grads(pre_gate, pre_up, sigma, grad_hidden):
    grad_up = grad_hidden * (pre_gate * sigma)
    grad_gate = grad_hidden * pre_up * sigma * (1.0 + pre_gate * (1.0 - sigma))
    return grad_gate.astype(BF16), grad_up.astype(BF16)


def forward_kernel(capacity, win_in, x_ref, slots_in, gates_in, back0, back1, wg_ref, wu_ref, wd_ref,
                   mix_ref, out_ref, hid_ref):
    step = pl.program_id(0)
    for sub in range(TOK // SUB):
        part = slice(sub * SUB, (sub + 1) * SUB)
        total = combine_rows(step * (TOK // SUB) + sub, sub, win_in, slots_in, gates_in, (back0, back1), capacity)
        mix_ref[part, :] = (x_ref[part, :].astype(F32) + total).astype(BF16)
    rows = mix_ref[...]
    for at in range(0, wg_ref.shape[1], CHUNK):
        cols = slice(at, at + CHUNK)
        pre_gate = dot(rows, wg_ref[:, cols])
        pre_up = dot(rows, wu_ref[:, cols])
        hid_ref[:, cols] = (pre_gate * jax.nn.sigmoid(pre_gate) * pre_up).astype(BF16)
    out_ref[...] = (rows.astype(F32) + dot(hid_ref[...], wd_ref[...])).astype(BF16)


def top_kernel(capacity, win_in, x_ref, gy_ref, slots_in, gates_in, back0, back1, wg_ref, wu_ref, wd_ref,
               y_ref, grad_ref, hid_ref, dg_ref, du_ref, mix_ref):
    step = pl.program_id(0)
    for sub in range(TOK // SUB):
        part = slice(sub * SUB, (sub + 1) * SUB)
        total = combine_rows(step * (TOK // SUB) + sub, sub, win_in, slots_in, gates_in, (back0, back1), capacity)
        mix_ref[part, :] = (x_ref[part, :].astype(F32) + total).astype(BF16)
    rows = mix_ref[...]
    grad = gy_ref[...]
    for at in range(0, wg_ref.shape[1], CHUNK):
        cols = slice(at, at + CHUNK)
        pre_gate = dot(rows, wg_ref[:, cols])
        pre_up = dot(rows, wu_ref[:, cols])
        sigma = jax.nn.sigmoid(pre_gate)
        hid_ref[:, cols] = (pre_gate * sigma * pre_up).astype(BF16)
        grad_hidden = dot(grad, wd_ref[cols, :], LAST)
        dg_ref[:, cols], du_ref[:, cols] = swiglu_grads(pre_gate, pre_up, sigma, grad_hidden)
    y_ref[...] = (rows.astype(F32) + dot(hid_ref[...], wd_ref[...])).astype(BF16)
    branch = dot(dg_ref[...], wg_ref[...], LAST) + dot(du_ref[...], wu_ref[...], LAST)
    grad_ref[...] = (grad.astype(F32) + branch).astype(BF16)


def backward_kernel(capacity, win_in, g_ref, x_ref, slots_in, back0, back1, wg_ref, wu_ref, wd_ref,
                    grad_ref, dg_ref, du_ref, mix_ref):
    step = pl.program_id(0)
    for sub in range(TOK // SUB):
        part = slice(sub * SUB, (sub + 1) * SUB)
        total = combine_rows(step * (TOK // SUB) + sub, sub, win_in, slots_in, None, (back0, back1), capacity)
        mix_ref[part, :] = (g_ref[part, :].astype(F32) + total).astype(BF16)
    rows = x_ref[...]
    grad = mix_ref[...]
    for at in range(0, wg_ref.shape[1], CHUNK):
        cols = slice(at, at + CHUNK)
        pre_gate = dot(rows, wg_ref[:, cols])
        pre_up = dot(rows, wu_ref[:, cols])
        sigma = jax.nn.sigmoid(pre_gate)
        grad_hidden = dot(grad, wd_ref[cols, :], LAST)
        dg_ref[:, cols], du_ref[:, cols] = swiglu_grads(pre_gate, pre_up, sigma, grad_hidden)
    branch = dot(dg_ref[...], wg_ref[...], LAST) + dot(du_ref[...], wu_ref[...], LAST)
    grad_ref[...] = (grad.astype(F32) + branch).astype(BF16)


def final_kernel(capacity, win_in, g_ref, slots_in, back0, back1, out_ref):
    step = pl.program_id(0)
    for sub in range(TOK // SUB):
        part = slice(sub * SUB, (sub + 1) * SUB)
        total = combine_rows(step * (TOK // SUB) + sub, sub, win_in, slots_in, None, (back0, back1), capacity)
        out_ref[part, :] = (g_ref[part, :].astype(F32) + total).astype(BF16)


def pack_kernel(n_local, with_gates, win_ref, x_ref, slots_ref, *refs):
    gates_ref, refs = (refs[0], refs[1:]) if with_gates else (None, refs)
    sends, columns = refs[:n_local], refs[n_local:]
    step = pl.program_id(0)

    @pl.when(step == 0)
    def _():
        zero_all(refs)

    line = lax.broadcasted_iota(jnp.int32, (WIN, SUB), 0)
    subs = PACK // SUB

    def moved(sub):
        part = slice(sub * SUB, (sub + 1) * SUB)
        rows = x_ref[part, :]
        found = []
        for loc in range(n_local):
            window = (step * subs + sub) * n_local + loc
            match = line == slots_ref[loc:loc + 1, part] - win_ref[2 * window]
            target = pl.ds(pl.multiple_of(win_ref[2 * window + 1], 16), WIN)
            gate = jnp.where(match, gates_ref[loc:loc + 1, part], 0.0) if with_gates else None
            found.append((target, dot(jnp.where(match, 1.0, 0.0).astype(BF16), rows), gate))
        return found

    ready = moved(0)
    for sub in range(subs):
        following = moved(sub + 1) if sub + 1 < subs else None
        for loc, (target, rows, gate) in enumerate(ready):
            sends[loc][target, :] = (sends[loc][target, :].astype(F32) + rows).astype(BF16)
            if with_gates:
                columns[loc][target, :] += gate
        ready = following


def spread(meta, source, target, capacity):
    for src in range(target.shape[0] // capacity):
        at = pl.ds(pl.multiple_of(meta[1 + src], 16), capacity)
        target[src * capacity:(src + 1) * capacity, :] = source[at, :]


def expert_forward_kernel(capacity, meta, x_ref, w1_ref, w3_ref, w2_ref, o_ref, all_ref, hid_ref):
    step = pl.program_id(0)

    @pl.when(step == 0)
    def _():
        zero_all((all_ref,))

    @pl.when(step < meta[0])
    def _():
        rows = x_ref[...]
        for at in range(0, w1_ref.shape[1], CHUNK):
            cols = slice(at, at + CHUNK)
            pre_gate = dot(rows, w1_ref[:, cols])
            pre_up = dot(rows, w3_ref[:, cols])
            hid_ref[:, cols] = (pre_gate * jax.nn.sigmoid(pre_gate) * pre_up).astype(BF16)
        block = pl.ds(pl.multiple_of(step * ROWS, ROWS), ROWS)
        all_ref[block, :] = dot(hid_ref[...], w2_ref[...]).astype(BF16)

    @pl.when(step == pl.num_programs(0) - 1)
    def _():
        spread(meta, all_ref, o_ref, capacity)


def expert_backward_kernel(capacity, n_local, loc, meta, win_ref, x_ref, c_ref, gcol_ref, slots_ref,
                           w1_ref, w3_ref, w2_ref, dx_ref, dgate_ref, hid_ref, dg_ref, du_ref, all_ref, dcol_ref):
    step = pl.program_id(0)

    @pl.when(step == 0)
    def _():
        zero_all((all_ref, dcol_ref))

    @pl.when(step < meta[0])
    def _():
        block = pl.ds(pl.multiple_of(step * ROWS, ROWS), ROWS)
        rows = x_ref[...]
        grad = c_ref[...]
        gate = jnp.sum(gcol_ref[...], axis=1, keepdims=True)
        partial = jnp.zeros((ROWS, 128), F32)
        for at in range(0, w1_ref.shape[1], CHUNK):
            cols = slice(at, at + CHUNK)
            pre_gate = dot(rows, w1_ref[:, cols])
            pre_up = dot(rows, w3_ref[:, cols])
            sigma = jax.nn.sigmoid(pre_gate)
            hidden = (pre_gate * sigma * pre_up).astype(BF16)
            hid_ref[:, cols] = hidden
            back = dot(grad, w2_ref[cols, :], LAST)
            product = hidden.astype(F32) * back
            for lane in range(0, CHUNK, 128):
                partial += product[:, lane:lane + 128]
            dg_ref[:, cols], du_ref[:, cols] = swiglu_grads(pre_gate, pre_up, sigma, back * gate)
        dcol_ref[block, :] = partial
        all_ref[block, :] = (dot(dg_ref[...], w1_ref[...], LAST) + dot(du_ref[...], w3_ref[...], LAST)).astype(BF16)

    @pl.when(step == pl.num_programs(0) - 1)
    def _():
        spread(meta, all_ref, dx_ref, capacity)
        line = lax.broadcasted_iota(jnp.int32, (WIN, SUB), 0)
        n_src, n_tok = dgate_ref.shape
        for src in range(n_src):
            def body(sub, _):
                window = (src * (n_tok // SUB) + sub) * n_local + loc
                part = pl.ds(pl.multiple_of(sub * SUB, SUB), SUB)
                where = slots_ref[src:src + 1, part] - win_ref[2 * window]
                source = pl.ds(pl.multiple_of(win_ref[2 * window + 1], 16), WIN)
                values = jnp.sum(dcol_ref[source, :], axis=1, keepdims=True)
                dgate_ref[src:src + 1, part] = jnp.sum(jnp.where(line == where, values, 0.0), axis=0, keepdims=True)
                return 0

            lax.fori_loop(0, n_tok // SUB, body, 0)


def expert_weights_kernel(n_alias, meta, x_ref, c_ref, gcol_ref, hid_ref, dg_ref, du_ref, *refs):
    dw1_ref, dw3_ref, dw2_ref = refs[n_alias:]
    step = pl.program_id(0)

    @pl.when(step == 0)
    def _():
        zero_all((dw1_ref, dw3_ref, dw2_ref))

    @pl.when(step < meta[0])
    def _():
        gate = jnp.sum(gcol_ref[...], axis=1, keepdims=True)
        scaled = (c_ref[...].astype(F32) * gate).astype(BF16)
        rows = x_ref[...]
        dw1_ref[...] += dot(rows, dg_ref[...], FIRST)
        dw3_ref[...] += dot(rows, du_ref[...], FIRST)
        dw2_ref[...] += dot(hid_ref[...], scaled, FIRST)


def solution(mesh):
    group = mesh.shape['ep']
    tok_spec = P(('dp', 'ep'), None)
    exp_spec = P('ep', None, None)
    full_spec = P(None, None)
    grad_spec = P(('dp', 'ep'), None, None)
    buffered = pl.Buffered(buffer_count=1)

    def layer_program(x_in, grad_y, ids_a, gate_a, ids_b, gate_b, w1_a, w3_a, w2_a, w1_b, w3_b, w2_b,
                       wg_mid, wu_mid, wd_mid, wg_top, wu_top, wd_top):
        n_tok, dim = x_in.shape
        n_local, _, ff = w1_a.shape
        n_exp = n_local * group
        capacity = 2 * n_tok * ids_a.shape[1] // n_exp
        n_rows = group * capacity
        me = lax.axis_index('ep')

        tile = pl.BlockSpec((TOK, dim), lambda i, *_: (i, 0))
        col_tile = pl.BlockSpec((TOK, n_exp), lambda i, *_: (i, 0))
        whole = pl.BlockSpec((n_rows, dim), lambda i, *_: (0, 0), pipeline_mode=buffered)
        w_in = pl.BlockSpec((dim, ff), lambda i, *_: (0, 0), pipeline_mode=buffered)
        w_out = pl.BlockSpec((ff, dim), lambda i, *_: (0, 0), pipeline_mode=buffered)
        rows_shape = jax.ShapeDtypeStruct((n_tok, dim), BF16)
        buffer_shape = jax.ShapeDtypeStruct((n_rows, dim), BF16)
        wide = pltpu.VMEM((TOK, ff), BF16)
        narrow = pltpu.VMEM((TOK, dim), BF16)
        unit_flops = 2 * n_tok * dim * ff

        def token_call(kernel, in_specs, out_specs, out_shape, scratch, matmuls):
            return pl.pallas_call(
                functools.partial(kernel, capacity),
                grid_spec=pltpu.PrefetchScalarGridSpec(
                    num_scalar_prefetch=1, grid=(n_tok // TOK,), in_specs=in_specs, out_specs=out_specs,
                    scratch_shapes=scratch),
                out_shape=out_shape, compiler_params=params(),
                cost_estimate=cost(int(matmuls * unit_flops), 20 * 2**20))

        forward = token_call(forward_kernel, [tile, col_tile, col_tile, whole, whole, w_in, w_in, w_out],
                             [tile, tile], [rows_shape, rows_shape], [wide], 5)
        top = token_call(top_kernel, [tile, tile, col_tile, col_tile, whole, whole, w_in, w_in, w_out],
                         [tile, tile], [rows_shape, rows_shape], [wide, wide, wide, narrow], 8)
        backward = token_call(backward_kernel, [tile, tile, col_tile, whole, whole, w_in, w_in, w_out],
                              tile, rows_shape, [wide, wide, narrow], 7)
        final = token_call(final_kernel, [tile, col_tile, whole, whole], tile, rows_shape, [], 1)

        n_blocks = n_rows // ROWS
        tiles = n_tok // PACK
        pack_tile = pl.BlockSpec((PACK, dim), lambda i, *_: (i, 0))
        line = pl.BlockSpec((None, n_local, PACK), lambda i, *_: (i // tiles, 0, i % tiles))
        column_shape = jax.ShapeDtypeStruct((n_rows, 128), F32)
        column = pl.BlockSpec((n_rows, 128), lambda i, *_: (0, 0), pipeline_mode=buffered)

        def pack(windows, tokens, slots, gates=None):
            with_gates = gates is not None
            return pl.pallas_call(
                functools.partial(pack_kernel, n_local, with_gates),
                grid_spec=pltpu.PrefetchScalarGridSpec(
                    num_scalar_prefetch=1, grid=(group * tiles,),
                    in_specs=[pack_tile, line] + [line] * with_gates,
                    out_specs=[whole] * n_local + [column] * (n_local * with_gates)),
                out_shape=[buffer_shape] * n_local + [column_shape] * (n_local * with_gates),
                compiler_params=params(), cost_estimate=cost(2 * unit_flops, 20 * 2**20),
            )(windows, tokens, slots, *((gates,) if with_gates else ()))

        def row_block(i, meta, *_):
            return (jnp.maximum(jnp.minimum(i, meta[0] - 1), 0), 0)

        def expert_specs(loc):
            return (pl.BlockSpec((ROWS, dim), row_block),
                    pl.BlockSpec((None, dim, ff), lambda i, *_: (loc, 0, 0), pipeline_mode=buffered),
                    pl.BlockSpec((None, ff, dim), lambda i, *_: (loc, 0, 0), pipeline_mode=buffered))

        def expert_forward(loc, meta, tokens, w1, w3, w2):
            block, e_in, e_out = expert_specs(loc)
            return pl.pallas_call(
                functools.partial(expert_forward_kernel, capacity),
                grid_spec=pltpu.PrefetchScalarGridSpec(
                    num_scalar_prefetch=1, grid=(n_blocks,), in_specs=[block, e_in, e_in, e_out], out_specs=whole,
                    scratch_shapes=[pltpu.VMEM((n_rows, dim), BF16), pltpu.VMEM((ROWS, ff), BF16)]),
                out_shape=buffer_shape, compiler_params=params(),
                cost_estimate=cost(3 * unit_flops, 12 * 2**20))(meta, tokens, w1, w3, w2)

        hidden_block = pl.BlockSpec((ROWS, ff), row_block)
        hidden_shape = jax.ShapeDtypeStruct((n_rows, ff), BF16)

        def expert_backward(loc, meta, windows, tokens, grads, gates, slots, w1, w3, w2):
            block, e_in, e_out = expert_specs(loc)
            small = pl.BlockSpec((group, n_tok), lambda i, *_: (0, 0), pipeline_mode=buffered)
            return pl.pallas_call(
                functools.partial(expert_backward_kernel, capacity, n_local, loc),
                grid_spec=pltpu.PrefetchScalarGridSpec(
                    num_scalar_prefetch=2, grid=(n_blocks,),
                    in_specs=[block, block, pl.BlockSpec((ROWS, 128), row_block), small, e_in, e_in, e_out],
                    out_specs=[whole, small] + [hidden_block] * 3,
                    scratch_shapes=[pltpu.VMEM((n_rows, dim), BF16), pltpu.VMEM((n_rows, 128), F32)]),
                out_shape=[buffer_shape, jax.ShapeDtypeStruct((group, n_tok), F32)] + [hidden_shape] * 3,
                compiler_params=params(), cost_estimate=cost(5 * unit_flops, 60 * 2**20),
            )(meta, windows, tokens, grads, gates, slots, w1, w3, w2)

        def expert_weights(loc, meta, tokens, grads, gates, hidden, earlier):
            block, e_in, e_out = expert_specs(loc)
            n_alias = 0 if earlier is None else 3
            aliases = {} if earlier is None else {7: 0, 8: 1, 9: 2}
            extra = () if earlier is None else tuple(earlier)
            return pl.pallas_call(
                functools.partial(expert_weights_kernel, n_alias),
                grid_spec=pltpu.PrefetchScalarGridSpec(
                    num_scalar_prefetch=1, grid=(n_blocks,),
                    in_specs=([block, block, pl.BlockSpec((ROWS, 128), row_block)] + [hidden_block] * 3
                              + [pl.BlockSpec(memory_space=pl.ANY)] * n_alias),
                    out_specs=[e_in, e_in, e_out]),
                out_shape=[jax.ShapeDtypeStruct((n_local, dim, ff), F32), jax.ShapeDtypeStruct((n_local, dim, ff), F32),
                           jax.ShapeDtypeStruct((n_local, ff, dim), F32)],
                input_output_aliases=aliases, compiler_params=params(),
                cost_estimate=cost(3 * unit_flops, 60 * 2**20),
            )(meta, tokens, grads, gates, *hidden, *extra)

        ids_both, gates_both = jnp.stack([ids_a, ids_b]), jnp.stack([gate_a, gate_b])
        slots_here, gates_here, starts_here, _ = route(ids_both, gates_both, jnp.arange(n_exp, dtype=jnp.int32))
        windows_here = jnp.minimum(starts_here // 16 * 16, capacity - WIN)
        win_a, win_b = windows_here.transpose(0, 2, 1).reshape(2, -1)
        slots_col, gates_col = slots_here.transpose(0, 2, 1), gates_here.transpose(0, 2, 1)
        ids_all = lax.all_gather(ids_both, 'ep')
        gates_all = lax.all_gather(gates_both, 'ep')
        slots, gates, starts, counts = route(ids_all, gates_all, me * n_local + jnp.arange(n_local, dtype=jnp.int32))
        room = (counts + 15) // 16 * 16
        offsets = jnp.cumsum(room, axis=0) - room
        windows = jnp.minimum(starts // 16 * 16, capacity - WIN)
        windows = jnp.stack([windows, windows + offsets[..., None]], axis=-1)
        windows = windows.transpose(1, 0, 3, 2, 4).reshape(2, -1)
        n_used = (jnp.sum(room, axis=0) + ROWS - 1) // ROWS
        meta = jnp.concatenate([n_used[None], offsets], axis=0)

        def gather_rows(rows):
            return lax.all_gather(rows, 'ep', axis=0, tiled=True)

        def to_home(rows):
            return lax.all_to_all(rows.reshape(group, capacity, dim), 'ep', 0, 0, tiled=True).reshape(n_rows, dim)

        def moe_forward(tokens, layer, w1, w3, w2):
            backs = []
            for loc in range(n_local):
                rows = expert_forward(loc, meta[:, layer, loc], tokens[loc], w1, w3, w2)
                if backs:
                    rows, backs[-1] = lax.optimization_barrier((rows, backs[-1]))
                backs.append(to_home(rows))
            return backs

        def moe_backward(tokens, grads, layer, ids, w1, w3, w2):
            backs, dgates, kept, earlier = [], [], [], None
            packed = pack(windows[layer], grads, slots[:, layer], gates[:, layer])
            for loc in range(n_local):
                dx, dgate, *hidden = expert_backward(
                    loc, meta[:, layer, loc], windows[layer], tokens[loc], packed[loc], packed[n_local + loc],
                    slots[:, layer, loc], w1, w3, w2)
                if backs:
                    dx, backs[-1] = lax.optimization_barrier((dx, backs[-1]))
                backs.append(to_home(dx))
                dgates.append(dgate)
                kept.append(hidden)
            for loc in range(n_local):
                earlier = expert_weights(loc, meta[:, layer, loc], tokens[loc], packed[loc], packed[n_local + loc],
                                         kept[loc], earlier)
            dgates, backs = lax.optimization_barrier((jnp.stack(dgates, axis=1), backs))
            home = lax.all_to_all(dgates, 'ep', 0, 0, tiled=True)
            experts = jnp.arange(n_exp, dtype=jnp.int32)[:, None, None]
            dgate = jnp.sum(jnp.where(ids[None] == experts, home.reshape(n_exp, n_tok)[:, :, None], 0.0), axis=0)
            return backs, dgate, earlier

        tokens_a = pack(windows[0], gather_rows(x_in), slots[:, 0])
        backs_a = moe_forward(tokens_a, 0, w1_a, w3_a, w2_a)
        x_a, x_mid = forward(win_a, x_in, slots_col[0], gates_col[0], *backs_a, wg_mid, wu_mid, wd_mid)
        tokens_b = pack(windows[1], gather_rows(x_mid), slots[:, 1])
        backs_b = moe_forward(tokens_b, 1, w1_b, w3_b, w2_b)

        y_out, grad_b = top(win_b, x_mid, grad_y, slots_col[1], gates_col[1], *backs_b, wg_top, wu_top, wd_top)
        again, _ = lax.optimization_barrier((x_in, grad_b))
        backs_b, dgate_b, dw_b = moe_backward(tokens_b, gather_rows(grad_b), 1, ids_b, w1_b, w3_b, w2_b)
        tokens_a = pack(windows[0], gather_rows(again), slots[:, 0])
        grad_a = backward(win_b, grad_b, x_a, slots_col[1], *backs_b, wg_mid, wu_mid, wd_mid)
        backs_a, dgate_a, dw_a = moe_backward(tokens_a, gather_rows(grad_a), 0, ids_a, w1_a, w3_a, w2_a)
        dx_in = final(win_a, grad_a, slots_col[0], *backs_a)
        return (y_out, dx_in, *dw_a, *dw_b, dgate_a, dgate_b)

    in_specs = (tok_spec, tok_spec, tok_spec, tok_spec, tok_spec, tok_spec,
                exp_spec, exp_spec, exp_spec, exp_spec, exp_spec, exp_spec,
                full_spec, full_spec, full_spec, full_spec, full_spec, full_spec)
    out_specs = (tok_spec, tok_spec, grad_spec, grad_spec, grad_spec, grad_spec, grad_spec, grad_spec, tok_spec, tok_spec)
    return jax.shard_map(layer_program, mesh=mesh, in_specs=in_specs, out_specs=out_specs, check_vma=False)
```

time: 1870 us -> 1090 us (0.58)
  matrix products: 726 us -> 0 us
  Pallas kernels: 0 us -> 589 us
  local copies, waits for them, and re-layouts: 535 us -> 16.2 us
  blocking collectives: 195 us -> 12.1 us
  waiting for transfers between devices: 217 us -> 376 us
  other arithmetic: 139 us -> 23.2 us
    dot_general x30 -> x0, matrix products: 726 us -> none  [the longest x2 128 us: expert_backward(): jnp.einsum('secd,efd->secf', grad_out, w_two, preferred_element_type=jnp....]
    pallas_call x0 -> x21, Pallas kernels: none -> 589 us  [the longest x4 191 us: expert_backward(): pl.pallas_call(functools.partial(expert_backward_kernel, capacity, n_loca...]
    gather x12 -> x0, local copies, waits for them, and re-layouts: 367 us -> none  [the longest x4 143 us: send_rows(): picked = jnp.take(rows, filler // top_k, axis=0, mode='fill', fill_value=0)]
    all_to_all x2 -> x0, blocking collectives: 195 us -> none  [send_rows(): lax.all_to_all(picked.reshape(group, n_local, capacity, hidden_dim), 'ep'...]
    all_gather x0 -> x5, waiting for transfers between devices: none -> 193 us  [gather_rows(): return lax.all_gather(rows, 'ep', axis=0, tiled=True)]
    reduce_sum x8 -> x3, other arithmetic: 79.4 us -> 1.47 us  [the longest x2 1.31 us: moe_backward(): jnp.sum(jnp.where(ids[None] == experts, home.reshape(n_exp, n_tok)[:, :,...]
    convert_element_type x8 -> x0, local copies, waits for them, and re-layouts: 71.8 us -> none  [the longest x2 21.2 us: moe_backward(): jnp.sum(grad_pairs, axis=1, dtype=jnp.float32)]
    all_to_all x10, waiting for transfers between devices: 217 us -> 183 us  [the longest x8 183 us: to_home(): lax.all_to_all(rows.reshape(group, capacity, dim), 'ep', 0, 0, tiled=True)]
  transfers between devices with their start and end apart: 10 -> 15, of which waited for: 4 -> 10; matrix products, arithmetic and copies ran while one was open for 49% -> 4% of each run, Pallas kernels for 0% -> 37%
where the time goes in v1:
time: 1090 us; the launch traced here: 1080 us
  Pallas kernels  589 us (54%)
  waiting for transfers between devices  376 us (34%)
  starting transfers between devices  47.1 us (4%)
  other arithmetic  23.2 us (2%)
  local copies, waits for them, and re-layouts  16.2 us (1%)
  between operations  14.4 us (1%)
  blocking collectives  12.1 us (1%)
    all_gather x5, waiting for transfers between devices, gather_rows(): return lax.all_gather(rows, 'ep', axis=0, tiled=True)  193 us
    pallas_call x4, Pallas kernels, expert_backward(): pl.pallas_call(functools.partial(expert_backward_kernel, capacity, n_loca...  191 us
    all_to_all x8, waiting for transfers between devices, to_home(): lax.all_to_all(rows.reshape(group, capacity, dim), 'ep', 0, 0, tiled=True)  183 us
    pallas_call x4, Pallas kernels, expert_weights(): pl.pallas_call(functools.partial(expert_weights_kernel, n_alias), grid_sp...  114 us
    pallas_call x4, Pallas kernels, expert_forward(): pl.pallas_call(functools.partial(expert_forward_kernel, capacity), grid_s...  99.6 us
    pallas_call x5, Pallas kernels, pack(): pl.pallas_call(functools.partial(pack_kernel, n_local, with_gates), grid_...  72.5 us
    all_to_all x8, starting transfers between devices, to_home(): lax.all_to_all(rows.reshape(group, capacity, dim), 'ep', 0, 0, tiled=True)  39.6 us
    pallas_call x1, Pallas kernels, layer_program(): top(win_b, x_mid, grad_y, slots_col[1], gates_col[1], *backs_b, wg_top, w...  39.1 us
  transfers between devices with their start and end apart: 15, of which 10 were waited for; matrix products, arithmetic and copies ran while one was open for 4% of the time, Pallas kernels for 37%

profile of v1, /device:TPU:0, one launch (start us, length us, event | category | flops | bytes accessed | tf_op | source)
XLA Modules:
  0.0 1077.6 jit_solution(10894601929103967550)
XLA Ops:
  8.7 6.7 all-gather
  15.6 4.6 reduce-window.16
  26.5 42.3 %all-gather.8.cloned.1.call-done.x_ref = bf16[8192,512]{1,0:T(8,128)(2,1)} async-done(((bf16[2048,512]{1,0:T(8,128)(2,1)}), bf16[8192,512]{1,0:T(8,128)(2,1)}) %all-gather.8.cloned.1.call-update) | async-done | bytes 8388624 | tf_op jit(solution)/shard_map/all_gather | solution.py:409
  68.7 13.6 %shard_map.249 = (bf16[4096,512]{1,0:T(8,128)(2,1)}, bf16[4096,512]{1,0:T(8,128)(2,1)}) custom-call(s32[256]{0:T(256)} %squeeze.78.win_ref, bf16[8192,512]{1,0:T(8,128)(2,1)} %all-gather.8.cloned.1.call-done.x_ref, s32[4,2,2048]{2,1,0:T(2,128)} %copy.120.slots_ref), custom_call_target="tpu_custom_call" | custom-call | flops 7516192768 | bytes 20971520 | tf_op jit(solution)/shard_map/pallas_call | solution.py:329
  82.4 19.3 %shard_map.251 = bf16[4096,512]{1,0:T(8,128)(2,1)} custom-call(s32[5]{0:T(128)} %get-tuple-element.176.meta, bf16[4096,512]{1,0:T(8,128)(2,1)} %get-tuple-element.76.x_ref, bf16[2,512,1792]{2,1,0:T(8,128)(2,1)} %w1_ref.15, bf16[2,512,1792]{2,1,0:T(8,128)(2,1)} %w3_ref.15, bf16[2,1792,512]{2,1,0:T(8,128)(2,1)} %w2_ref.15), custom_call_target="tpu_custom_call" | custom-call | flops 11274289152 | bytes 12582912 | tf_op jit(solution)/shard_map/pallas_call | solution.py:349
  101.7 5.0 all-to-all-start
  106.8 4.6 reduce-window.14
  112.2 1.9 copy.108
  114.2 25.7 %shard_map.250 = bf16[4096,512]{1,0:T(8,128)(2,1)} custom-call(s32[5]{0:T(128)} %get-tuple-element.175.meta, bf16[4096,512]{1,0:T(8,128)(2,1)} %get-tuple-element.75.x_ref, bf16[2,512,1792]{2,1,0:T(8,128)(2,1)} %w1_ref.15, bf16[2,512,1792]{2,1,0:T(8,128)(2,1)} %w3_ref.15, bf16[2,1792,512]{2,1,0:T(8,128)(2,1)} %w2_ref.15), custom_call_target="tpu_custom_call" | custom-call | flops 11274289152 | bytes 12582912 | tf_op jit(solution)/shard_map/pallas_call | solution.py:349
  139.9 15.0 %all-to-all-done = bf16[4,1024,512]{2,1,0:T(8,128)(2,1)} async-done(((bf16[4,1024,512]{2,1,0:T(8,128)(2,1)}), bf16[4,1024,512]{2,1,0:T(8,128)(2,1)}, u32[]{:S(2)}, u32[]{:S(2)}) %all-to-all-start) | async-done | bytes 4194336 | tf_op jit(solution)/shard_map/all_to_all | solution.py:412
  154.9 4.9 all-to-all-start.1
  160.0 5.4 select_bitcast_fusion
  167.7 2.3 select_add_fusion
  172.9 35.0 %all-to-all-done.1 = bf16[4,1024,512]{2,1,0:T(8,128)(2,1)} async-done(((bf16[4,1024,512]{2,1,0:T(8,128)(2,1)}), bf16[4,1024,512]{2,1,0:T(8,128)(2,1)}, u32[]{:S(2)}, u32[]{:S(2)}) %all-to-all-start.1) | async-done | bytes 4194336 | tf_op jit(solution)/shard_map/all_to_all | solution.py:412
  208.0 26.4 %shard_map.252 = (bf16[2048,512]{1,0:T(8,128)(2,1)}, bf16[2048,512]{1,0:T(8,128)(2,1)}) custom-call(s32[128]{0:T(128)} %unstack.15.win_in, bf16[2048,512]{1,0:T(8,128)(2,1)} %x_ref.1, s32[2048,8]{1,0:T(8,128)} %get-tuple-element.149.slots_in, f32[2048,8]{1,0:T(8,128)} %get-tuple-element.147.gates_in, bf16[4096,512]{1,0:T(8,128)(2,1)} %bitcast.23.back0, ...), custom_call_target="tpu_custom_call" | custom-call | flops 18790481920 | bytes 20971520 | tf_op jit(solution)/shard_map/pallas_call | solution.py:446
  235.9 60.5 %all-gather.10.cloned.1.call-done.x_ref = bf16[8192,512]{1,0:T(8,128)(2,1)} async-done(((bf16[2048,512]{1,0:T(8,128)(2,1)}), bf16[8192,512]{1,0:T(8,128)(2,1)}) %all-gather.10.cloned.1.call-update) | async-done | bytes 8388624 | tf_op jit(solution)/shard_map/all_gather | solution.py:409
  296.4 13.6 %shard_map.253 = (bf16[4096,512]{1,0:T(8,128)(2,1)}, bf16[4096,512]{1,0:T(8,128)(2,1)}) custom-call(s32[256]{0:T(256)} %squeeze.84.win_ref, bf16[8192,512]{1,0:T(8,128)(2,1)} %all-gather.10.cloned.1.call-done.x_ref, s32[4,2,2048]{2,1,0:T(2,128)} %copy.122.slots_ref), custom_call_target="tpu_custom_call" | custom-call | flops 7516192768 | bytes 20971520 | tf_op jit(solution)/shard_map/pallas_call | solution.py:329
  310.0 25.7 %shard_map.255 = bf16[4096,512]{1,0:T(8,128)(2,1)} custom-call(s32[5]{0:T(128)} %get-tuple-element.174.meta, bf16[4096,512]{1,0:T(8,128)(2,1)} %get-tuple-element.81.x_ref, bf16[2,512,1792]{2,1,0:T(8,128)(2,1)} %w1_ref.13, bf16[2,512,1792]{2,1,0:T(8,128)(2,1)} %w3_ref.13, bf16[2,1792,512]{2,1,0:T(8,128)(2,1)} %w2_ref.13), custom_call_target="tpu_custom_call" | custom-call | flops 11274289152 | bytes 12582912 | tf_op jit(solution)/shard_map/pallas_call | solution.py:349
  335.7 4.9 all-to-all-start.2
  340.6 28.9 %shard_map.254 = bf16[4096,512]{1,0:T(8,128)(2,1)} custom-call(s32[5]{0:T(128)} %get-tuple-element.177.meta, bf16[4096,512]{1,0:T(8,128)(2,1)} %get-tuple-element.80.x_ref, bf16[2,512,1792]{2,1,0:T(8,128)(2,1)} %w1_ref.13, bf16[2,512,1792]{2,1,0:T(8,128)(2,1)} %w3_ref.13, bf16[2,1792,512]{2,1,0:T(8,128)(2,1)} %w2_ref.13), custom_call_target="tpu_custom_call" | custom-call | flops 11274289152 | bytes 12582912 | tf_op jit(solution)/shard_map/pallas_call | solution.py:349
  369.4 19.3 %all-to-all-done.2 = bf16[4,1024,512]{2,1,0:T(8,128)(2,1)} async-done(((bf16[4,1024,512]{2,1,0:T(8,128)(2,1)}), bf16[4,1024,512]{2,1,0:T(8,128)(2,1)}, u32[]{:S(2)}, u32[]{:S(2)}) %all-to-all-start.2) | async-done | bytes 4194336 | tf_op jit(solution)/shard_map/all_to_all | solution.py:412
  388.8 4.9 all-to-all-start.3
  394.5 47.3 %all-to-all-done.3 = bf16[4,1024,512]{2,1,0:T(8,128)(2,1)} async-done(((bf16[4,1024,512]{2,1,0:T(8,128)(2,1)}), bf16[4,1024,512]{2,1,0:T(8,128)(2,1)}, u32[]{:S(2)}, u32[]{:S(2)}) %all-to-all-start.3) | async-done | bytes 4194336 | tf_op jit(solution)/shard_map/all_to_all | solution.py:412
  441.8 39.1 %shard_map.256 = (bf16[2048,512]{1,0:T(8,128)(2,1)}, bf16[2048,512]{1,0:T(8,128)(2,1)}) custom-call(s32[128]{0:T(128)} %unstack.13.win_in, bf16[2048,512]{1,0:T(8,128)(2,1)} %get-tuple-element.79.x_ref, bf16[2048,512]{1,0:T(8,128)(2,1)} %gy_ref.1, s32[2048,8]{1,0:T(8,128)} %get-tuple-element.148.slots_in, f32[2048,8]{1,0:T(8,128)} %get-tuple-element.146.gates_in, ...), custom_call_target="tpu_custom_call" | custom-call | flops 30064771072 | bytes 20971520 | tf_op jit(solution)/shard_map/pallas_call | solution.py:450
  481.0 5.4 all-gather.1
  488.1 50.1 %all-gather.12.cloned.1.call-done.x_ref = bf16[8192,512]{1,0:T(8,128)(2,1)} async-done(((bf16[2048,512]{1,0:T(8,128)(2,1)}), bf16[8192,512]{1,0:T(8,128)(2,1)}) %all-gather.12.cloned.1.call-update) | async-done | bytes 8388624 | tf_op jit(solution)/shard_map/all_gather | solution.py:409
  538.2 15.7 %shard_map.257 = (bf16[4096,512]{1,0:T(8,128)(2,1)}, bf16[4096,512]{1,0:T(8,128)(2,1)}, f32[4096,128]{1,0:T(8,128)}, f32[4096,128]{1,0:T(8,128)}) custom-call(s32[256]{0:T(256)} %squeeze.84.win_ref, bf16[8192,512]{1,0:T(8,128)(2,1)} %all-gather.12.cloned.1.call-done.x_ref, s32[4,2,2048]{2,1,0:T(2,128)} %copy.122.slots_ref, f32[4,2,2048]{2,1,0:T(2,128)} %copy.126.refs_0_), custom_call_target="tpu_custom_call" | custom-call | flops 7516192768 | bytes 20971520 | tf_op jit(solution)/shard_map/pallas_call | solution.py:329
  553.9 49.2 %shard_map.258 = (bf16[4096,512]{1,0:T(8,128)(2,1)}, f32[4,2048]{1,0:T(4,128)}, bf16[4096,1792]{1,0:T(8,128)(2,1)}, bf16[4096,1792]{1,0:T(8,128)(2,1)}, bf16[4096,1792]{1,0:T(8,128)(2,1)}) custom-call(s32[5]{0:T(128)} %get-tuple-element.174.meta, s32[256]{0:T(256)} %squeeze.84.win_ref, bf16[4096,512]{1,0:T(8,128)(2,1)} %get-tuple-element.81.x_ref, ...), custom_call_target="tpu_custom_call" | custom-call | flops 18790481920 | bytes 62914560 | tf_op jit(solution)/shard_map/pallas_call | solution.py:363
  603.2 4.9 all-to-all-start.4
  608.0 54.8 %shard_map.259 = (bf16[4096,512]{1,0:T(8,128)(2,1)}, f32[4,2048]{1,0:T(4,128)}, bf16[4096,1792]{1,0:T(8,128)(2,1)}, bf16[4096,1792]{1,0:T(8,128)(2,1)}, bf16[4096,1792]{1,0:T(8,128)(2,1)}) custom-call(s32[5]{0:T(128)} %get-tuple-element.177.meta, s32[256]{0:T(256)} %squeeze.84.win_ref, bf16[4096,512]{1,0:T(8,128)(2,1)} %get-tuple-element.80.x_ref, ...), custom_call_target="tpu_custom_call" | custom-call | flops 18790481920 | bytes 62914560 | tf_op jit(solution)/shard_map/pallas_call | solution.py:363
  662.9 5.0 all-to-all-start.5
  668.4 47.7 %all-to-all-done.5 = bf16[4,1024,512]{2,1,0:T(8,128)(2,1)} async-done(((bf16[4,1024,512]{2,1,0:T(8,128)(2,1)}), bf16[4,1024,512]{2,1,0:T(8,128)(2,1)}, u32[]{:S(2)}, u32[]{:S(2)}) %all-to-all-start.5) | async-done | bytes 4194336 | tf_op jit(solution)/shard_map/all_to_all | solution.py:412
  716.1 33.1 %shard_map.260.g_ref = bf16[2048,512]{1,0:T(8,128)(2,1)} custom-call(s32[128]{0:T(128)} %unstack.13.win_in, bf16[2048,512]{1,0:T(8,128)(2,1)} %get-tuple-element.85.g_ref, bf16[2048,512]{1,0:T(8,128)(2,1)} %get-tuple-element.86.x_ref, s32[2048,8]{1,0:T(8,128)} %get-tuple-element.148.slots_in, bf16[4096,512]{1,0:T(8,128)(2,1)} %bitcast.44.back0, ...), custom_call_target="tpu_custom_call" | custom-call | flops 26306674688 | bytes 20971520 | tf_op jit(solution)/shard_map/pallas_call | solution.py:454
  749.9 14.2 %shard_map.261 = (bf16[4096,512]{1,0:T(8,128)(2,1)}, bf16[4096,512]{1,0:T(8,128)(2,1)}) custom-call(s32[256]{0:T(256)} %squeeze.78.win_ref, bf16[8192,512]{1,0:T(8,128)(2,1)} %all-gather.14.cloned.1.call-done.x_ref, s32[4,2,2048]{2,1,0:T(2,128)} %copy.120.slots_ref), custom_call_target="tpu_custom_call" | custom-call | flops 7516192768 | bytes 20971520 | tf_op jit(solution)/shard_map/pallas_call | solution.py:329
  764.1 39.7 %all-gather.16.cloned.1.call-done.x_ref = bf16[8192,512]{1,0:T(8,128)(2,1)} async-done(((bf16[2048,512]{1,0:T(8,128)(2,1)}), bf16[8192,512]{1,0:T(8,128)(2,1)}) %all-gather.16.cloned.1.call-update) | async-done | bytes 8388624 | tf_op jit(solution)/shard_map/all_gather | solution.py:409
  803.8 15.3 %shard_map.262 = (bf16[4096,512]{1,0:T(8,128)(2,1)}, bf16[4096,512]{1,0:T(8,128)(2,1)}, f32[4096,128]{1,0:T(8,128)}, f32[4096,128]{1,0:T(8,128)}) custom-call(s32[256]{0:T(256)} %squeeze.78.win_ref, bf16[8192,512]{1,0:T(8,128)(2,1)} %all-gather.16.cloned.1.call-done.x_ref, s32[4,2,2048]{2,1,0:T(2,128)} %copy.120.slots_ref, f32[4,2,2048]{2,1,0:T(2,128)} %copy.129.refs_0_), custom_call_target="tpu_custom_call" | custom-call | flops 7516192768 | bytes 20971520 | tf_op jit(solution)/shard_map/pallas_call | solution.py:329
  819.1 38.2 %shard_map.263 = (bf16[4096,512]{1,0:T(8,128)(2,1)}, f32[4,2048]{1,0:T(4,128)}, bf16[4096,1792]{1,0:T(8,128)(2,1)}, bf16[4096,1792]{1,0:T(8,128)(2,1)}, bf16[4096,1792]{1,0:T(8,128)(2,1)}) custom-call(s32[5]{0:T(128)} %get-tuple-element.176.meta, s32[256]{0:T(256)} %squeeze.78.win_ref, bf16[4096,512]{1,0:T(8,128)(2,1)} %get-tuple-element.100.x_ref, ...), custom_call_target="tpu_custom_call" | custom-call | flops 18790481920 | bytes 62914560 | tf_op jit(solution)/shard_map/pallas_call | solution.py:363
  857.3 5.0 all-to-all-start.6
  862.3 29.4 %shard_map.268 = (f32[2,512,1792]{2,1,0:T(8,128)}, f32[2,512,1792]{2,1,0:T(8,128)}, f32[2,1792,512]{2,1,0:T(8,128)}) custom-call(s32[5]{0:T(128)} %get-tuple-element.174.meta, bf16[4096,512]{1,0:T(8,128)(2,1)} %get-tuple-element.81.x_ref, bf16[4096,512]{1,0:T(8,128)(2,1)} %get-tuple-element.87.c_ref, f32[4096,128]{1,0:T(8,128)} %get-tuple-element.88.gcol_ref, ...), custom_call_target="tpu_custom_call" | custom-call | flops 11274289152 | bytes 62914560 | tf_op jit(solution)/shard_map/pallas_call | solution.py:379
  892.4 18.1 %all-to-all-done.6 = bf16[4,1024,512]{2,1,0:T(8,128)(2,1)} async-done(((bf16[4,1024,512]{2,1,0:T(8,128)(2,1)}), bf16[4,1024,512]{2,1,0:T(8,128)(2,1)}, u32[]{:S(2)}, u32[]{:S(2)}) %all-to-all-start.6) | async-done | bytes 4194336 | tf_op jit(solution)/shard_map/all_to_all | solution.py:412
  910.5 3.3 all-to-all-start.9
  913.8 49.2 %shard_map.264 = (bf16[4096,512]{1,0:T(8,128)(2,1)}, f32[4,2048]{1,0:T(4,128)}, bf16[4096,1792]{1,0:T(8,128)(2,1)}, bf16[4096,1792]{1,0:T(8,128)(2,1)}, bf16[4096,1792]{1,0:T(8,128)(2,1)}) custom-call(s32[5]{0:T(128)} %get-tuple-element.175.meta, s32[256]{0:T(256)} %squeeze.78.win_ref, bf16[4096,512]{1,0:T(8,128)(2,1)} %get-tuple-element.104.x_ref, ...), custom_call_target="tpu_custom_call" | custom-call | flops 18790481920 | bytes 62914560 | tf_op jit(solution)/shard_map/pallas_call | solution.py:363
  963.0 5.1 all-to-all-start.7
  968.1 33.0 %shard_map.269 = (f32[2,512,1792]{2,1,0:T(8,128)}, f32[2,512,1792]{2,1,0:T(8,128)}, f32[2,1792,512]{2,1,0:T(8,128)}) custom-call(s32[5]{0:T(128)} %get-tuple-element.177.meta, bf16[4096,512]{1,0:T(8,128)(2,1)} %get-tuple-element.80.x_ref, bf16[4096,512]{1,0:T(8,128)(2,1)} %get-tuple-element.90.c_ref, ...), custom_call_target="tpu_custom_call", output_to_operand_aliasing={{0}: (7, {}), {1}: (8, {}), {2}: (9, {})} | custom-call | flops 11274289152 | bytes 62914560 | tf_op jit(solution)/shard_map/pallas_call | solution.py:379
  1001.8 22.6 %shard_map.266 = (f32[2,512,1792]{2,1,0:T(8,128)}, f32[2,512,1792]{2,1,0:T(8,128)}, f32[2,1792,512]{2,1,0:T(8,128)}) custom-call(s32[5]{0:T(128)} %get-tuple-element.176.meta, bf16[4096,512]{1,0:T(8,128)(2,1)} %get-tuple-element.100.x_ref, bf16[4096,512]{1,0:T(8,128)(2,1)} %get-tuple-element.101.c_ref, f32[4096,128]{1,0:T(8,128)} %get-tuple-element.102.gcol_ref, ...), custom_call_target="tpu_custom_call" | custom-call | flops 11274289152 | bytes 62914560 | tf_op jit(solution)/shard_map/pallas_call | solution.py:379
  1024.4 29.4 %shard_map.267 = (f32[2,512,1792]{2,1,0:T(8,128)}, f32[2,512,1792]{2,1,0:T(8,128)}, f32[2,1792,512]{2,1,0:T(8,128)}) custom-call(s32[5]{0:T(128)} %get-tuple-element.175.meta, bf16[4096,512]{1,0:T(8,128)(2,1)} %get-tuple-element.104.x_ref, bf16[4096,512]{1,0:T(8,128)(2,1)} %get-tuple-element.105.c_ref, ...), custom_call_target="tpu_custom_call", output_to_operand_aliasing={{0}: (7, {}), {1}: (8, {}), {2}: (9, {})} | custom-call | flops 11274289152 | bytes 62914560 | tf_op jit(solution)/shard_map/pallas_call | solution.py:379
  1054.5 3.3 all-to-all-start.8
  1057.8 12.3 %shard_map.265 = bf16[2048,512]{1,0:T(8,128)(2,1)} custom-call(s32[128]{0:T(128)} %unstack.15.win_in, bf16[2048,512]{1,0:T(8,128)(2,1)} %shard_map.260.g_ref, s32[2048,8]{1,0:T(8,128)} %get-tuple-element.149.slots_in, bf16[4096,512]{1,0:T(8,128)(2,1)} %bitcast.53.back0, bf16[4096,512]{1,0:T(8,128)(2,1)} %bitcast.55.back1), custom_call_target="tpu_custom_call" | custom-call | flops 3758096384 | bytes 20971520 | tf_op jit(solution)/shard_map/pallas_call | solution.py:456
  (98 shorter events, 22.4 us)
Async XLA Ops:
  7.2 61.6 %all-gather.8.cloned.1.call-start = ((), (), s32[]{:S(2)}) async-start(), calls=%async_computation.10 | async-start | bytes 10485760 | tf_op jit(solution)/shard_map/all_gather | solution.py:409
  101.7 5.0 copy-start
  101.7 5.0 copy-start.2
  101.7 53.2 %all-to-all-start = ((bf16[4,1024,512]{2,1,0:T(8,128)(2,1)}), bf16[4,1024,512]{2,1,0:T(8,128)(2,1)}, u32[]{:S(2)}, u32[]{:S(2)}) async-start(bf16[4,1024,512]{2,1,0:T(8,128)(2,1)} %bitcast.101), calls=%async_computation | async-start | bytes 8388608 | tf_op jit(solution)/shard_map/all_to_all | solution.py:412
  154.9 53.1 %all-to-all-start.1 = ((bf16[4,1024,512]{2,1,0:T(8,128)(2,1)}), bf16[4,1024,512]{2,1,0:T(8,128)(2,1)}, u32[]{:S(2)}, u32[]{:S(2)}) async-start(bf16[4,1024,512]{2,1,0:T(8,128)(2,1)} %bitcast.100), calls=%async_computation.1 | async-start | bytes 8388608 | tf_op jit(solution)/shard_map/all_to_all | solution.py:412
  159.8 7.9 copy-start.4
  159.8 7.9 copy-start.5
  159.8 136.6 %all-gather.10.cloned.1.call-start = ((), (), s32[]{:S(2)}) async-start(), calls=%async_computation.11 | async-start | bytes 10485760 | tf_op jit(solution)/shard_map/all_gather | solution.py:409
  335.7 53.1 %all-to-all-start.2 = ((bf16[4,1024,512]{2,1,0:T(8,128)(2,1)}), bf16[4,1024,512]{2,1,0:T(8,128)(2,1)}, u32[]{:S(2)}, u32[]{:S(2)}) async-start(bf16[4,1024,512]{2,1,0:T(8,128)(2,1)} %bitcast.106), calls=%async_computation.2 | async-start | bytes 8388608 | tf_op jit(solution)/shard_map/all_to_all | solution.py:412
  388.8 53.1 %all-to-all-start.3 = ((bf16[4,1024,512]{2,1,0:T(8,128)(2,1)}), bf16[4,1024,512]{2,1,0:T(8,128)(2,1)}, u32[]{:S(2)}, u32[]{:S(2)}) async-start(bf16[4,1024,512]{2,1,0:T(8,128)(2,1)} %bitcast.105), calls=%async_computation.3 | async-start | bytes 8388608 | tf_op jit(solution)/shard_map/all_to_all | solution.py:412
  393.6 144.5 %all-gather.12.cloned.1.call-start = ((), (), s32[]{:S(2)}) async-start(), calls=%async_computation.12 | async-start | bytes 10485760 | tf_op jit(solution)/shard_map/all_gather | solution.py:409
  480.9 268.9 %all-gather.14.cloned.1.call-start = ((), (), s32[]{:S(2)}) async-start(), calls=%async_computation.13 | async-start | bytes 10485760 | tf_op jit(solution)/shard_map/all_gather | solution.py:409
  603.2 59.7 %all-to-all-start.4 = ((bf16[4,1024,512]{2,1,0:T(8,128)(2,1)}), bf16[4,1024,512]{2,1,0:T(8,128)(2,1)}, u32[]{:S(2)}, u32[]{:S(2)}) async-start(bf16[4,1024,512]{2,1,0:T(8,128)(2,1)} %bitcast.104), calls=%async_computation.4 | async-start | bytes 8388608 | tf_op jit(solution)/shard_map/all_to_all | solution.py:412
  662.8 5.5 copy-start.8
  662.8 5.5 copy-start.9
  662.9 53.2 %all-to-all-start.5 = ((bf16[4,1024,512]{2,1,0:T(8,128)(2,1)}), bf16[4,1024,512]{2,1,0:T(8,128)(2,1)}, u32[]{:S(2)}, u32[]{:S(2)}) async-start(bf16[4,1024,512]{2,1,0:T(8,128)(2,1)} %bitcast.103), calls=%async_computation.5 | async-start | bytes 8388608 | tf_op jit(solution)/shard_map/all_to_all | solution.py:412
  667.9 135.9 %all-gather.16.cloned.1.call-start = ((), (), s32[]{:S(2)}) async-start(), calls=%async_computation.14 | async-start | bytes 10485760 | tf_op jit(solution)/shard_map/all_gather | solution.py:409
  857.3 53.2 %all-to-all-start.6 = ((bf16[4,1024,512]{2,1,0:T(8,128)(2,1)}), bf16[4,1024,512]{2,1,0:T(8,128)(2,1)}, u32[]{:S(2)}, u32[]{:S(2)}) async-start(bf16[4,1024,512]{2,1,0:T(8,128)(2,1)} %bitcast.102), calls=%async_computation.6 | async-start | bytes 8388608 | tf_op jit(solution)/shard_map/all_to_all | solution.py:412
  910.5 52.5 %all-to-all-start.9 = ((f32[4,2,2048]{2,1,0:T(2,128)}), f32[4,2,2048]{2,1,0:T(2,128)S(1)}, u32[]{:S(2)}, u32[]{:S(2)}) async-start(f32[4,2,2048]{2,1,0:T(2,128)} %copy.131), calls=%async_computation.9 | async-start | bytes 131072 | tf_op jit(solution)/shard_map/all_to_all | solution.py:439
  963.0 90.8 %all-to-all-start.7 = ((bf16[4,1024,512]{2,1,0:T(8,128)(2,1)}), bf16[4,1024,512]{2,1,0:T(8,128)(2,1)}, u32[]{:S(2)}, u32[]{:S(2)}) async-start(bf16[4,1024,512]{2,1,0:T(8,128)(2,1)} %bitcast.99), calls=%async_computation.7 | async-start | bytes 8388608 | tf_op jit(solution)/shard_map/all_to_all | solution.py:412
  968.1 33.1 %copy-start.1 = (s32[2048,2]{0,1:T(2,128)S(1)}, s32[2048,2]{0,1:T(2,128)}, u32[]{:S(2)}) copy-start(s32[2048,2]{0,1:T(2,128)} %param.22) | copy-start | bytes 49156
  968.1 33.7 %copy-start.6 = (f32[4,2048]{1,0:T(4,128)S(1)}, f32[4,2048]{1,0:T(4,128)}, u32[]{:S(2)}) copy-start(f32[4,2048]{1,0:T(4,128)} %get-tuple-element.103) | copy-start | bytes 98308
  968.1 33.7 %copy-start.7 = (f32[4,2048]{1,0:T(4,128)S(1)}, f32[4,2048]{1,0:T(4,128)}, u32[]{:S(2)}) copy-start(f32[4,2048]{1,0:T(4,128)} %get-tuple-element.107) | copy-start | bytes 98308
  1054.5 15.6 %all-to-all-start.8 = ((f32[4,2,2048]{2,1,0:T(2,128)}), f32[4,2,2048]{2,1,0:T(2,128)S(1)}, u32[]{:S(2)}, u32[]{:S(2)}) async-start(f32[4,2,2048]{2,1,0:T(2,128)} %copy.130), calls=%async_computation.8 | async-start | bytes 131072 | tf_op jit(solution)/shard_map/all_to_all | solution.py:439
  1057.8 12.4 %copy-start.3 = (s32[2048,2]{0,1:T(2,128)S(1)}, s32[2048,2]{0,1:T(2,128)}, u32[]{:S(2)}) copy-start(s32[2048,2]{0,1:T(2,128)} %param.20) | copy-start | bytes 49156
Sparse Core Ops, SparseCore 0:
  9.5 59.1 all-gather.7
  234.5 61.8 all-gather.9
  481.1 57.0 all-gather.11
  539.6 56.4 all-gather.13
  749.3 54.3 all-gather.15

commit v2 on v1

--- a/solution.py
+++ b/solution.py
@@ -93,12 +93,12 @@
     out_ref[...] = (rows.astype(F32) + dot(hid_ref[...], wd_ref[...])).astype(BF16)
 
 
-def top_kernel(capacity, win_in, x_ref, gy_ref, slots_in, gates_in, back0, back1, wg_ref, wu_ref, wd_ref,
+def top_kernel(capacity, win_in, x_ref, gy_ref, slots_in, gates_in, back, wg_ref, wu_ref, wd_ref,
                y_ref, grad_ref, hid_ref, dg_ref, du_ref, mix_ref):
     step = pl.program_id(0)
     for sub in range(TOK // SUB):
         part = slice(sub * SUB, (sub + 1) * SUB)
-        total = combine_rows(step * (TOK // SUB) + sub, sub, win_in, slots_in, gates_in, (back0, back1), capacity)
+        total = combine_rows(step * (TOK // SUB) + sub, sub, win_in, slots_in, gates_in, (back,), capacity)
         mix_ref[part, :] = (x_ref[part, :].astype(F32) + total).astype(BF16)
     rows = mix_ref[...]
     grad = gy_ref[...]
@@ -143,9 +143,9 @@
         out_ref[part, :] = (g_ref[part, :].astype(F32) + total).astype(BF16)
 
 
-def pack_kernel(n_local, with_gates, win_ref, x_ref, slots_ref, *refs):
+def pack_kernel(n_local, n_sends, with_gates, win_ref, x_ref, slots_ref, *refs):
     gates_ref, refs = (refs[0], refs[1:]) if with_gates else (None, refs)
-    sends, columns = refs[:n_local], refs[n_local:]
+    sends, columns = refs[:n_sends], refs[n_sends:]
     step = pl.program_id(0)
 
     @pl.when(step == 0)
@@ -171,7 +171,8 @@
     for sub in range(subs):
         following = moved(sub + 1) if sub + 1 < subs else None
         for loc, (target, rows, gate) in enumerate(ready):
-            sends[loc][target, :] = (sends[loc][target, :].astype(F32) + rows).astype(BF16)
+            send = sends[loc % n_sends]
+            send[target, :] = (send[target, :].astype(F32) + rows).astype(BF16)
             if with_gates:
                 columns[loc][target, :] += gate
         ready = following
@@ -204,6 +205,28 @@
     @pl.when(step == pl.num_programs(0) - 1)
     def _():
         spread(meta, all_ref, o_ref, capacity)
+
+
+def all_experts_kernel(capacity, plan, x_ref, w1_ref, w3_ref, w2_ref, o_ref, hid_ref):
+    step = pl.program_id(0)
+    parts, depth, ff = w1_ref.shape
+    out_depth, dim = w2_ref.shape[1:]
+
+    @pl.when(step == 0)
+    def _():
+        zero_all((o_ref,))
+
+    @pl.when(step < plan[0])
+    def _():
+        rows = x_ref[...]
+        for at in range(0, ff, CHUNK):
+            cols = slice(at, at + CHUNK)
+            pre_gate = dot(rows, w1_ref[:, :, cols].reshape(parts * depth, CHUNK))
+            pre_up = dot(rows, w3_ref[:, :, cols].reshape(parts * depth, CHUNK))
+            hid_ref[:, cols] = (pre_gate * jax.nn.sigmoid(pre_gate) * pre_up).astype(BF16)
+        at = plan[1 + 2 * step] * capacity + plan[2 + 2 * step] * ROWS
+        o_ref[pl.ds(pl.multiple_of(at, ROWS), ROWS), :] = dot(
+            hid_ref[...], w2_ref[...].reshape(parts * out_depth, dim)).astype(BF16)
 
 
 def expert_backward_kernel(capacity, n_local, loc, meta, win_ref, x_ref, c_ref, gcol_ref, slots_ref,
@@ -292,6 +315,7 @@
         tile = pl.BlockSpec((TOK, dim), lambda i, *_: (i, 0))
         col_tile = pl.BlockSpec((TOK, n_exp), lambda i, *_: (i, 0))
         whole = pl.BlockSpec((n_rows, dim), lambda i, *_: (0, 0), pipeline_mode=buffered)
+        pair_rows = pl.BlockSpec((n_exp * capacity, dim), lambda i, *_: (0, 0), pipeline_mode=buffered)
         w_in = pl.BlockSpec((dim, ff), lambda i, *_: (0, 0), pipeline_mode=buffered)
         w_out = pl.BlockSpec((ff, dim), lambda i, *_: (0, 0), pipeline_mode=buffered)
         rows_shape = jax.ShapeDtypeStruct((n_tok, dim), BF16)
@@ -311,7 +335,7 @@
 
         forward = token_call(forward_kernel, [tile, col_tile, col_tile, whole, whole, w_in, w_in, w_out],
                              [tile, tile], [rows_shape, rows_shape], [wide], 5)
-        top = token_call(top_kernel, [tile, tile, col_tile, col_tile, whole, whole, w_in, w_in, w_out],
+        top = token_call(top_kernel, [tile, tile, col_tile, col_tile, pair_rows, w_in, w_in, w_out],
                          [tile, tile], [rows_shape, rows_shape], [wide, wide, wide, narrow], 8)
         backward = token_call(backward_kernel, [tile, tile, col_tile, whole, whole, w_in, w_in, w_out],
                               tile, rows_shape, [wide, wide, narrow], 7)
@@ -327,7 +351,7 @@
         def pack(windows, tokens, slots, gates=None):
             with_gates = gates is not None
             return pl.pallas_call(
-                functools.partial(pack_kernel, n_local, with_gates),
+                functools.partial(pack_kernel, n_local, n_local, with_gates),
                 grid_spec=pltpu.PrefetchScalarGridSpec(
                     num_scalar_prefetch=1, grid=(group * tiles,),
                     in_specs=[pack_tile, line] + [line] * with_gates,
@@ -389,10 +413,57 @@
                 cost_estimate=cost(3 * unit_flops, 60 * 2**20),
             )(meta, tokens, grads, gates, *hidden, *extra)
 
+        parts = mesh.shape['dp']
+        pair_shape = jax.ShapeDtypeStruct((n_exp * capacity, dim), BF16)
+        max_steps = n_tok * ids_a.shape[1] // ROWS + n_exp
+
+        def pack_pairs(windows, tokens, slots):
+            return pl.pallas_call(
+                functools.partial(pack_kernel, n_exp, 1, False),
+                grid_spec=pltpu.PrefetchScalarGridSpec(
+                    num_scalar_prefetch=1, grid=(tiles,),
+                    in_specs=[pack_tile, pl.BlockSpec((n_exp, PACK), lambda i, *_: (0, i))], out_specs=[pair_rows]),
+                out_shape=[pair_shape], compiler_params=params(), cost_estimate=cost(2 * unit_flops, 12 * 2**20),
+            )(windows, tokens, slots)[0]
+
+        def all_experts(plan, pairs, w1, w3, w2):
+            def pair_block(i, plan):
+                return (plan[1 + 2 * i] * (capacity // ROWS) + plan[2 + 2 * i], 0)
+
+            def weights(w):
+                return pl.BlockSpec((parts, None, None) + w.shape[3:],
+                                    lambda i, plan: (0, plan[1 + 2 * i] // n_local, plan[1 + 2 * i] % n_local, 0, 0))
+
+            return pl.pallas_call(
+                functools.partial(all_experts_kernel, capacity),
+                grid_spec=pltpu.PrefetchScalarGridSpec(
+                    num_scalar_prefetch=1, grid=(max_steps,),
+                    in_specs=[pl.BlockSpec((ROWS, dim), pair_block), weights(w1), weights(w3), weights(w2)],
+                    out_specs=pair_rows, scratch_shapes=[pltpu.VMEM((ROWS, ff), BF16)]),
+                out_shape=pair_shape, compiler_params=params(),
+                cost_estimate=cost(6 * unit_flops, 60 * 2**20))(plan, pairs, w1, w3, w2)
+
+        def block_plan(counts):
+            blocks = (counts + ROWS - 1) // ROWS
+            ends = jnp.cumsum(blocks)
+            index = jnp.minimum(jnp.arange(max_steps, dtype=jnp.int32), ends[-1] - 1)
+            passed = (index[:, None] >= ends[None, :]).astype(jnp.int32)
+            expert = jnp.sum(passed, axis=1)
+            block = index - jnp.sum(passed * blocks[None, :], axis=1)
+            return jnp.concatenate([ends[-1:], jnp.stack([expert, block], axis=1).reshape(-1)])
+
+        def gather_weights(w):
+            depth = w.shape[1] // parts
+            mine = lax.dynamic_slice_in_dim(w, lax.axis_index('dp') * depth, depth, 1)
+            return lax.all_gather(mine, ('dp', 'ep')).reshape((parts, group) + mine.shape)
+
         ids_both, gates_both = jnp.stack([ids_a, ids_b]), jnp.stack([gate_a, gate_b])
-        slots_here, gates_here, starts_here, _ = route(ids_both, gates_both, jnp.arange(n_exp, dtype=jnp.int32))
+        slots_here, gates_here, starts_here, counts_here = route(ids_both, gates_both, jnp.arange(n_exp, dtype=jnp.int32))
         windows_here = jnp.minimum(starts_here // 16 * 16, capacity - WIN)
         win_a, win_b = windows_here.transpose(0, 2, 1).reshape(2, -1)
+        base_b = (jnp.arange(n_exp, dtype=jnp.int32) * capacity)[:, None]
+        win_pairs = jnp.stack([windows_here[1], windows_here[1] + base_b], axis=-1).transpose(1, 0, 2).reshape(-1)
+        plan_b = block_plan(counts_here[1])
         slots_col, gates_col = slots_here.transpose(0, 2, 1), gates_here.transpose(0, 2, 1)
         ids_all = lax.all_gather(ids_both, 'ep')
         gates_all = lax.all_gather(gates_both, 'ep')
@@ -441,13 +512,16 @@
             dgate = jnp.sum(jnp.where(ids[None] == experts, home.reshape(n_exp, n_tok)[:, :, None], 0.0), axis=0)
             return backs, dgate, earlier
 
-        tokens_a = pack(windows[0], gather_rows(x_in), slots[:, 0])
+        x_all = gather_rows(x_in)
+        x_all, windows, *own_b = lax.optimization_barrier((x_all, windows, w1_b, w3_b, w2_b))
+        all_b = [gather_weights(w) for w in own_b]
+        tokens_a = pack(windows[0], x_all, slots[:, 0])
         backs_a = moe_forward(tokens_a, 0, w1_a, w3_a, w2_a)
         x_a, x_mid = forward(win_a, x_in, slots_col[0], gates_col[0], *backs_a, wg_mid, wu_mid, wd_mid)
+        pairs_b = all_experts(plan_b, pack_pairs(win_pairs, x_mid, slots_here[1]), *all_b)
+
+        y_out, grad_b = top(win_b, x_mid, grad_y, slots_col[1], gates_col[1], pairs_b, wg_top, wu_top, wd_top)
         tokens_b = pack(windows[1], gather_rows(x_mid), slots[:, 1])
-        backs_b = moe_forward(tokens_b, 1, w1_b, w3_b, w2_b)
-
-        y_out, grad_b = top(win_b, x_mid, grad_y, slots_col[1], gates_col[1], *backs_b, wg_top, wu_top, wd_top)
         again, _ = lax.optimization_barrier((x_in, grad_b))
         backs_b, dgate_b, dw_b = moe_backward(tokens_b, gather_rows(grad_b), 1, ids_b, w1_b, w3_b, w2_b)
         tokens_a = pack(windows[0], gather_rows(again), slots[:, 0])

time: 1090 us -> 1040 us (0.954)
  waiting for transfers between devices: 376 us -> 312 us
    all_gather x5, waiting for transfers between devices: 193 us -> 119 us  [gather_rows(): return lax.all_gather(rows, 'ep', axis=0, tiled=True)]
    pallas_call x6 -> x8, Pallas kernels: 112 us -> 169 us  [the longest x5 73 us: pack(): pl.pallas_call(functools.partial(pack_kernel, n_local, n_local, with_gate...]
    pallas_call x4 -> x2, Pallas kernels: 99.6 us -> 45.5 us  [expert_forward(): pl.pallas_call(functools.partial(expert_forward_kernel, capacity), grid_s...]
    all_gather x0 -> x3, waiting for transfers between devices: none -> 20.4 us  [gather_weights(): lax.all_gather(mine, ('dp', 'ep')).reshape((parts, group) + mine.shape)]
    all_to_all x8 -> x6, waiting for transfers between devices: 183 us -> 172 us  [to_home(): lax.all_to_all(rows.reshape(group, capacity, dim), 'ep', 0, 0, tiled=True)]
    all_to_all x8 -> x6, starting transfers between devices: 39.6 us -> 29.8 us  [to_home(): lax.all_to_all(rows.reshape(group, capacity, dim), 'ep', 0, 0, tiled=True)]
  transfers between devices with their start and end apart: 15 -> 16, of which waited for: 10 -> 8; matrix products, arithmetic and copies ran while one was open for 4% -> 5% of each run, Pallas kernels for 37% -> 53%
where the time goes in v2:
time: 1040 us; the launch traced here: 1020 us
  Pallas kernels  593 us (57%)
  waiting for transfers between devices  312 us (30%)
  starting transfers between devices  37.2 us (4%)
  local copies, waits for them, and re-layouts  26.6 us (3%)
  other arithmetic  26.3 us (3%)
  between operations  15.5 us (1%)
  blocking collectives  12.3 us (1%)
    pallas_call x4, Pallas kernels, expert_backward(): pl.pallas_call(functools.partial(expert_backward_kernel, capacity, n_loca...  191 us
    all_to_all x6, waiting for transfers between devices, to_home(): lax.all_to_all(rows.reshape(group, capacity, dim), 'ep', 0, 0, tiled=True)  172 us
    all_gather x5, waiting for transfers between devices, gather_rows(): return lax.all_gather(rows, 'ep', axis=0, tiled=True)  119 us
    pallas_call x4, Pallas kernels, expert_weights(): pl.pallas_call(functools.partial(expert_weights_kernel, n_alias), grid_sp...  114 us
    pallas_call x5, Pallas kernels, pack(): pl.pallas_call(functools.partial(pack_kernel, n_local, n_local, with_gate...  73 us
    pallas_call x2, Pallas kernels, expert_forward(): pl.pallas_call(functools.partial(expert_forward_kernel, capacity), grid_s...  45.5 us
    pallas_call x1, Pallas kernels, all_experts(): pl.pallas_call(functools.partial(all_experts_kernel, capacity), grid_spec...  45.3 us
    pallas_call x1, Pallas kernels, layer_program(): top(win_b, x_mid, grad_y, slots_col[1], gates_col[1], pairs_b, wg_top, wu...  39.1 us
  transfers between devices with their start and end apart: 16, of which 8 were waited for; matrix products, arithmetic and copies ran while one was open for 5% of the time, Pallas kernels for 53%

profile of v2, /device:TPU:0, one launch (start us, length us, event | category | flops | bytes accessed | tf_op | source)
XLA Modules:
  0.0 1023.0 jit_solution(15801741904437166938)
XLA Ops:
  8.7 6.7 all-gather
  15.6 4.6 reduce-window.20
  24.6 44.2 %all-gather.14.cloned.1.call-done.x_ref = bf16[8192,512]{1,0:T(8,128)(2,1)} async-done(((bf16[2048,512]{1,0:T(8,128)(2,1)}), bf16[8192,512]{1,0:T(8,128)(2,1)}) %all-gather.14.cloned.1.call-update) | async-done | bytes 8388624 | tf_op jit(solution)/shard_map/all_gather | solution.py:480
  68.7 2.2 constant_dynamic-slice_fusion
  71.0 2.2 constant_dynamic-slice_fusion.2
  73.2 2.2 constant_dynamic-slice_fusion.1
  77.5 13.8 %shard_map.249 = (bf16[4096,512]{1,0:T(8,128)(2,1)}, bf16[4096,512]{1,0:T(8,128)(2,1)}) custom-call(s32[256]{0:T(256)} %bitcast.159, bf16[8192,512]{1,0:T(8,128)(2,1)} %all-gather.14.cloned.1.call-done.x_ref, s32[4,2,2048]{2,1,0:T(2,128)} %copy.129.slots_ref), custom_call_target="tpu_custom_call" | custom-call | flops 7516192768 | bytes 20971520 | tf_op jit(solution)/shard_map/pallas_call | solution.py:353
  91.3 19.7 %shard_map.251 = bf16[4096,512]{1,0:T(8,128)(2,1)} custom-call(s32[5]{0:T(128)} %get-tuple-element.182.meta, bf16[4096,512]{1,0:T(8,128)(2,1)} %get-tuple-element.81.x_ref, bf16[2,512,1792]{2,1,0:T(8,128)(2,1)} %w1_ref.11, bf16[2,512,1792]{2,1,0:T(8,128)(2,1)} %w3_ref.11, bf16[2,1792,512]{2,1,0:T(8,128)(2,1)} %w2_ref.11), custom_call_target="tpu_custom_call" | custom-call | flops 11274289152 | bytes 12582912 | tf_op jit(solution)/shard_map/pallas_call | solution.py:373
  111.0 5.0 all-to-all-start
  116.1 4.6 reduce-window.16
  121.5 1.9 copy.117
  123.5 25.8 %shard_map.250 = bf16[4096,512]{1,0:T(8,128)(2,1)} custom-call(s32[5]{0:T(128)} %get-tuple-element.181.meta, bf16[4096,512]{1,0:T(8,128)(2,1)} %get-tuple-element.80.x_ref, bf16[2,512,1792]{2,1,0:T(8,128)(2,1)} %w1_ref.11, bf16[2,512,1792]{2,1,0:T(8,128)(2,1)} %w3_ref.11, bf16[2,1792,512]{2,1,0:T(8,128)(2,1)} %w2_ref.11), custom_call_target="tpu_custom_call" | custom-call | flops 11274289152 | bytes 12582912 | tf_op jit(solution)/shard_map/pallas_call | solution.py:373
  149.3 40.5 %all-to-all-done = bf16[4,1024,512]{2,1,0:T(8,128)(2,1)} async-done(((bf16[4,1024,512]{2,1,0:T(8,128)(2,1)}), bf16[4,1024,512]{2,1,0:T(8,128)(2,1)}, u32[]{:S(2)}, u32[]{:S(2)}) %all-to-all-start) | async-done | bytes 4194336 | tf_op jit(solution)/shard_map/all_to_all | solution.py:483
  189.8 4.9 all-to-all-start.1
  194.9 5.4 fusion.1
  200.3 2.4 slice.143
  203.3 2.3 select_add_fusion
  208.6 66.2 %all-to-all-done.1 = bf16[4,1024,512]{2,1,0:T(8,128)(2,1)} async-done(((bf16[4,1024,512]{2,1,0:T(8,128)(2,1)}), bf16[4,1024,512]{2,1,0:T(8,128)(2,1)}, u32[]{:S(2)}, u32[]{:S(2)}) %all-to-all-start.1) | async-done | bytes 4194336 | tf_op jit(solution)/shard_map/all_to_all | solution.py:483
  274.8 27.3 %shard_map.252 = (bf16[2048,512]{1,0:T(8,128)(2,1)}, bf16[2048,512]{1,0:T(8,128)(2,1)}) custom-call(s32[128]{0:T(128)} %unstack.15.win_in, bf16[2048,512]{1,0:T(8,128)(2,1)} %x_ref.1, s32[2048,8]{1,0:T(8,128)} %get-tuple-element.157.slots_in, f32[2048,8]{1,0:T(8,128)} %get-tuple-element.155.gates_in, bf16[4096,512]{1,0:T(8,128)(2,1)} %bitcast.24.back0, ...), custom_call_target="tpu_custom_call" | custom-call | flops 18790481920 | bytes 20971520 | tf_op jit(solution)/shard_map/pallas_call | solution.py:520
  310.4 11.3 %shard_map.253.x_ref = bf16[8192,512]{1,0:T(8,128)(2,1)} custom-call(s32[256]{0:T(256)} %reshape.328.win_ref, bf16[2048,512]{1,0:T(8,128)(2,1)} %get-tuple-element.84.x_ref, s32[8,2048]{1,0:T(8,128)} %copy.133.slots_ref), custom_call_target="tpu_custom_call" | custom-call | flops 7516192768 | bytes 12582912 | tf_op jit(solution)/shard_map/pallas_call | solution.py:421
  321.8 20.4 %all-gather.26.cloned.1.call-done = bf16[32,128,1792]{2,1,0:T(8,128)(2,1)} async-done(((bf16[2,128,1792]{2,1,0:T(8,128)(2,1)}), bf16[32,128,1792]{2,1,0:T(8,128)(2,1)}) %all-gather.26.cloned.1.call-update) | async-done | bytes 14680080 | tf_op jit(solution)/shard_map/all_gather | solution.py:458
  342.2 45.3 %shard_map.254.back = bf16[8192,512]{1,0:T(8,128)(2,1)} custom-call(s32[49]{0:T(128)} %pad_add_fusion.3.plan, bf16[8192,512]{1,0:T(8,128)(2,1)} %shard_map.253.x_ref, bf16[4,4,2,128,1792]{4,3,2,1,0:T(8,128)(2,1)} %bitcast.170, bf16[4,4,2,128,1792]{4,3,2,1,0:T(8,128)(2,1)} %bitcast.171, bf16[4,4,2,448,512]{4,3,2,1,0:T(8,128)(2,1)} %bitcast.169), custom_call_target="tpu_custom_call" | custom-call | flops 22548578304 | bytes 62914560 | tf_op jit(solution)/shard_map/pallas_call | solution.py:437
  387.4 39.1 %shard_map.255 = (bf16[2048,512]{1,0:T(8,128)(2,1)}, bf16[2048,512]{1,0:T(8,128)(2,1)}) custom-call(s32[128]{0:T(128)} %unstack.13.win_in, bf16[2048,512]{1,0:T(8,128)(2,1)} %get-tuple-element.84.x_ref, bf16[2048,512]{1,0:T(8,128)(2,1)} %gy_ref.1, s32[2048,8]{1,0:T(8,128)} %get-tuple-element.156.slots_in, f32[2048,8]{1,0:T(8,128)} %get-tuple-element.154.gates_in, ...), custom_call_target="tpu_custom_call" | custom-call | flops 30064771072 | bytes 20971520 | tf_op jit(solution)/shard_map/pallas_call | solution.py:523
  426.6 5.6 all-gather.4
  434.6 13.9 %shard_map.256 = (bf16[4096,512]{1,0:T(8,128)(2,1)}, bf16[4096,512]{1,0:T(8,128)(2,1)}) custom-call(s32[256]{0:T(256)} %bitcast.164, bf16[8192,512]{1,0:T(8,128)(2,1)} %all-gather.16.cloned.1.call-done.x_ref, s32[4,2,2048]{2,1,0:T(2,128)} %copy.134.slots_ref), custom_call_target="tpu_custom_call" | custom-call | flops 7516192768 | bytes 20971520 | tf_op jit(solution)/shard_map/pallas_call | solution.py:353
  448.6 34.7 %all-gather.18.cloned.1.call-done.x_ref = bf16[8192,512]{1,0:T(8,128)(2,1)} async-done(((bf16[2048,512]{1,0:T(8,128)(2,1)}), bf16[8192,512]{1,0:T(8,128)(2,1)}) %all-gather.18.cloned.1.call-update) | async-done | bytes 8388624 | tf_op jit(solution)/shard_map/all_gather | solution.py:480
  483.2 15.8 %shard_map.257 = (bf16[4096,512]{1,0:T(8,128)(2,1)}, bf16[4096,512]{1,0:T(8,128)(2,1)}, f32[4096,128]{1,0:T(8,128)}, f32[4096,128]{1,0:T(8,128)}) custom-call(s32[256]{0:T(256)} %bitcast.165, bf16[8192,512]{1,0:T(8,128)(2,1)} %all-gather.18.cloned.1.call-done.x_ref, s32[4,2,2048]{2,1,0:T(2,128)} %copy.134.slots_ref, f32[4,2,2048]{2,1,0:T(2,128)} %copy.138.refs_0_), custom_call_target="tpu_custom_call" | custom-call | flops 7516192768 | bytes 20971520 | tf_op jit(solution)/shard_map/pallas_call | solution.py:353
  499.0 49.3 %shard_map.258 = (bf16[4096,512]{1,0:T(8,128)(2,1)}, f32[4,2048]{1,0:T(4,128)}, bf16[4096,1792]{1,0:T(8,128)(2,1)}, bf16[4096,1792]{1,0:T(8,128)(2,1)}, bf16[4096,1792]{1,0:T(8,128)(2,1)}) custom-call(s32[5]{0:T(128)} %get-tuple-element.180.meta, s32[256]{0:T(256)} %bitcast.166, bf16[4096,512]{1,0:T(8,128)(2,1)} %get-tuple-element.91.x_ref, ...), custom_call_target="tpu_custom_call" | custom-call | flops 18790481920 | bytes 62914560 | tf_op jit(solution)/shard_map/pallas_call | solution.py:387
  548.3 4.8 all-to-all-start.2
  553.1 54.8 %shard_map.259 = (bf16[4096,512]{1,0:T(8,128)(2,1)}, f32[4,2048]{1,0:T(4,128)}, bf16[4096,1792]{1,0:T(8,128)(2,1)}, bf16[4096,1792]{1,0:T(8,128)(2,1)}, bf16[4096,1792]{1,0:T(8,128)(2,1)}) custom-call(s32[5]{0:T(128)} %get-tuple-element.183.meta, s32[256]{0:T(256)} %bitcast.167, bf16[4096,512]{1,0:T(8,128)(2,1)} %get-tuple-element.95.x_ref, ...), custom_call_target="tpu_custom_call" | custom-call | flops 18790481920 | bytes 62914560 | tf_op jit(solution)/shard_map/pallas_call | solution.py:387
  607.9 5.0 all-to-all-start.3
  613.4 47.7 %all-to-all-done.3 = bf16[4,1024,512]{2,1,0:T(8,128)(2,1)} async-done(((bf16[4,1024,512]{2,1,0:T(8,128)(2,1)}), bf16[4,1024,512]{2,1,0:T(8,128)(2,1)}, u32[]{:S(2)}, u32[]{:S(2)}) %all-to-all-start.3) | async-done | bytes 4194336 | tf_op jit(solution)/shard_map/all_to_all | solution.py:483
  661.1 33.1 %shard_map.260.g_ref = bf16[2048,512]{1,0:T(8,128)(2,1)} custom-call(s32[128]{0:T(128)} %unstack.13.win_in, bf16[2048,512]{1,0:T(8,128)(2,1)} %get-tuple-element.89.g_ref, bf16[2048,512]{1,0:T(8,128)(2,1)} %get-tuple-element.90.x_ref, s32[2048,8]{1,0:T(8,128)} %get-tuple-element.156.slots_in, bf16[4096,512]{1,0:T(8,128)(2,1)} %bitcast.55.back0, ...), custom_call_target="tpu_custom_call" | custom-call | flops 26306674688 | bytes 20971520 | tf_op jit(solution)/shard_map/pallas_call | solution.py:528
  695.0 14.2 %shard_map.261 = (bf16[4096,512]{1,0:T(8,128)(2,1)}, bf16[4096,512]{1,0:T(8,128)(2,1)}) custom-call(s32[256]{0:T(256)} %bitcast.160, bf16[8192,512]{1,0:T(8,128)(2,1)} %all-gather.20.cloned.1.call-done.x_ref, s32[4,2,2048]{2,1,0:T(2,128)} %copy.129.slots_ref), custom_call_target="tpu_custom_call" | custom-call | flops 7516192768 | bytes 20971520 | tf_op jit(solution)/shard_map/pallas_call | solution.py:353
  709.1 39.7 %all-gather.22.cloned.1.call-done.x_ref = bf16[8192,512]{1,0:T(8,128)(2,1)} async-done(((bf16[2048,512]{1,0:T(8,128)(2,1)}), bf16[8192,512]{1,0:T(8,128)(2,1)}) %all-gather.22.cloned.1.call-update) | async-done | bytes 8388624 | tf_op jit(solution)/shard_map/all_gather | solution.py:480
  748.9 15.3 %shard_map.262 = (bf16[4096,512]{1,0:T(8,128)(2,1)}, bf16[4096,512]{1,0:T(8,128)(2,1)}, f32[4096,128]{1,0:T(8,128)}, f32[4096,128]{1,0:T(8,128)}) custom-call(s32[256]{0:T(256)} %bitcast.161, bf16[8192,512]{1,0:T(8,128)(2,1)} %all-gather.22.cloned.1.call-done.x_ref, s32[4,2,2048]{2,1,0:T(2,128)} %copy.129.slots_ref, f32[4,2,2048]{2,1,0:T(2,128)} %copy.141.refs_0_), custom_call_target="tpu_custom_call" | custom-call | flops 7516192768 | bytes 20971520 | tf_op jit(solution)/shard_map/pallas_call | solution.py:353
  764.2 38.2 %shard_map.263 = (bf16[4096,512]{1,0:T(8,128)(2,1)}, f32[4,2048]{1,0:T(4,128)}, bf16[4096,1792]{1,0:T(8,128)(2,1)}, bf16[4096,1792]{1,0:T(8,128)(2,1)}, bf16[4096,1792]{1,0:T(8,128)(2,1)}) custom-call(s32[5]{0:T(128)} %get-tuple-element.182.meta, s32[256]{0:T(256)} %bitcast.162, bf16[4096,512]{1,0:T(8,128)(2,1)} %get-tuple-element.106.x_ref, ...), custom_call_target="tpu_custom_call" | custom-call | flops 18790481920 | bytes 62914560 | tf_op jit(solution)/shard_map/pallas_call | solution.py:387
  802.4 5.0 all-to-all-start.4
  807.4 29.4 %shard_map.268 = (f32[2,512,1792]{2,1,0:T(8,128)}, f32[2,512,1792]{2,1,0:T(8,128)}, f32[2,1792,512]{2,1,0:T(8,128)}) custom-call(s32[5]{0:T(128)} %get-tuple-element.180.meta, bf16[4096,512]{1,0:T(8,128)(2,1)} %get-tuple-element.91.x_ref, bf16[4096,512]{1,0:T(8,128)(2,1)} %get-tuple-element.92.c_ref, f32[4096,128]{1,0:T(8,128)} %get-tuple-element.93.gcol_ref, ...), custom_call_target="tpu_custom_call" | custom-call | flops 11274289152 | bytes 62914560 | tf_op jit(solution)/shard_map/pallas_call | solution.py:403
  837.5 18.1 %all-to-all-done.4 = bf16[4,1024,512]{2,1,0:T(8,128)(2,1)} async-done(((bf16[4,1024,512]{2,1,0:T(8,128)(2,1)}), bf16[4,1024,512]{2,1,0:T(8,128)(2,1)}, u32[]{:S(2)}, u32[]{:S(2)}) %all-to-all-start.4) | async-done | bytes 4194336 | tf_op jit(solution)/shard_map/all_to_all | solution.py:483
  855.6 3.3 all-to-all-start.7
  858.9 49.2 %shard_map.264 = (bf16[4096,512]{1,0:T(8,128)(2,1)}, f32[4,2048]{1,0:T(4,128)}, bf16[4096,1792]{1,0:T(8,128)(2,1)}, bf16[4096,1792]{1,0:T(8,128)(2,1)}, bf16[4096,1792]{1,0:T(8,128)(2,1)}) custom-call(s32[5]{0:T(128)} %get-tuple-element.181.meta, s32[256]{0:T(256)} %bitcast.163, bf16[4096,512]{1,0:T(8,128)(2,1)} %get-tuple-element.110.x_ref, ...), custom_call_target="tpu_custom_call" | custom-call | flops 18790481920 | bytes 62914560 | tf_op jit(solution)/shard_map/pallas_call | solution.py:387
  908.1 5.1 all-to-all-start.5
  913.2 33.0 %shard_map.269 = (f32[2,512,1792]{2,1,0:T(8,128)}, f32[2,512,1792]{2,1,0:T(8,128)}, f32[2,1792,512]{2,1,0:T(8,128)}) custom-call(s32[5]{0:T(128)} %get-tuple-element.183.meta, bf16[4096,512]{1,0:T(8,128)(2,1)} %get-tuple-element.95.x_ref, bf16[4096,512]{1,0:T(8,128)(2,1)} %get-tuple-element.96.c_ref, ...), custom_call_target="tpu_custom_call", output_to_operand_aliasing={{0}: (7, {}), {1}: (8, {}), {2}: (9, {})} | custom-call | flops 11274289152 | bytes 62914560 | tf_op jit(solution)/shard_map/pallas_call | solution.py:403
  946.9 22.6 %shard_map.266 = (f32[2,512,1792]{2,1,0:T(8,128)}, f32[2,512,1792]{2,1,0:T(8,128)}, f32[2,1792,512]{2,1,0:T(8,128)}) custom-call(s32[5]{0:T(128)} %get-tuple-element.182.meta, bf16[4096,512]{1,0:T(8,128)(2,1)} %get-tuple-element.106.x_ref, bf16[4096,512]{1,0:T(8,128)(2,1)} %get-tuple-element.107.c_ref, f32[4096,128]{1,0:T(8,128)} %get-tuple-element.108.gcol_ref, ...), custom_call_target="tpu_custom_call" | custom-call | flops 11274289152 | bytes 62914560 | tf_op jit(solution)/shard_map/pallas_call | solution.py:403
  969.5 29.4 %shard_map.267 = (f32[2,512,1792]{2,1,0:T(8,128)}, f32[2,512,1792]{2,1,0:T(8,128)}, f32[2,1792,512]{2,1,0:T(8,128)}) custom-call(s32[5]{0:T(128)} %get-tuple-element.181.meta, bf16[4096,512]{1,0:T(8,128)(2,1)} %get-tuple-element.110.x_ref, bf16[4096,512]{1,0:T(8,128)(2,1)} %get-tuple-element.111.c_ref, ...), custom_call_target="tpu_custom_call", output_to_operand_aliasing={{0}: (7, {}), {1}: (8, {}), {2}: (9, {})} | custom-call | flops 11274289152 | bytes 62914560 | tf_op jit(solution)/shard_map/pallas_call | solution.py:403
  999.6 3.3 all-to-all-start.6
  1002.9 12.3 %shard_map.265 = bf16[2048,512]{1,0:T(8,128)(2,1)} custom-call(s32[128]{0:T(128)} %unstack.15.win_in, bf16[2048,512]{1,0:T(8,128)(2,1)} %shard_map.260.g_ref, s32[2048,8]{1,0:T(8,128)} %get-tuple-element.157.slots_in, bf16[4096,512]{1,0:T(8,128)(2,1)} %bitcast.64.back0, bf16[4096,512]{1,0:T(8,128)(2,1)} %bitcast.66.back1), custom_call_target="tpu_custom_call" | custom-call | flops 3758096384 | bytes 20971520 | tf_op jit(solution)/shard_map/pallas_call | solution.py:530
  (127 shorter events, 27.0 us)
Async XLA Ops:
  7.2 61.6 %all-gather.14.cloned.1.call-start = ((), (), s32[]{:S(2)}) async-start(), calls=%async_computation.8 | async-start | bytes 10485760 | tf_op jit(solution)/shard_map/all_gather | solution.py:480
  7.9 313.9 %all-gather.28.cloned.1.call-start = ((), (), s32[]{:S(2)}) async-start(), calls=%async_computation.15 | async-start | bytes 15597568 | tf_op jit(solution)/shard_map/all_gather | solution.py:458
  70.9 250.9 %all-gather.24.cloned.1.call-start = ((), (), s32[]{:S(2)}) async-start(), calls=%async_computation.13 | async-start | bytes 15597568 | tf_op jit(solution)/shard_map/all_gather | solution.py:458
  73.2 269.0 %all-gather.26.cloned.1.call-start = ((), (), s32[]{:S(2)}) async-start(), calls=%async_computation.14 | async-start | bytes 15597568 | tf_op jit(solution)/shard_map/all_gather | solution.py:458
  111.0 5.0 copy-start.1
  111.0 5.0 copy-start.3
  111.0 78.8 %all-to-all-start = ((bf16[4,1024,512]{2,1,0:T(8,128)(2,1)}), bf16[4,1024,512]{2,1,0:T(8,128)(2,1)}, u32[]{:S(2)}, u32[]{:S(2)}) async-start(bf16[4,1024,512]{2,1,0:T(8,128)(2,1)} %bitcast.132), calls=%async_computation | async-start | bytes 8388608 | tf_op jit(solution)/shard_map/all_to_all | solution.py:483
  189.8 85.0 %all-to-all-start.1 = ((bf16[4,1024,512]{2,1,0:T(8,128)(2,1)}), bf16[4,1024,512]{2,1,0:T(8,128)(2,1)}, u32[]{:S(2)}, u32[]{:S(2)}) async-start(bf16[4,1024,512]{2,1,0:T(8,128)(2,1)} %bitcast.131), calls=%async_computation.1 | async-start | bytes 8388608 | tf_op jit(solution)/shard_map/all_to_all | solution.py:483
  194.7 8.6 copy-start.5
  194.7 8.6 copy-start.6
  194.7 240.0 %all-gather.16.cloned.1.call-start = ((), (), s32[]{:S(2)}) async-start(), calls=%async_computation.9 | async-start | bytes 10485760 | tf_op jit(solution)/shard_map/all_gather | solution.py:480
  200.3 8.3 copy-start
  302.1 181.1 %all-gather.18.cloned.1.call-start = ((), (), s32[]{:S(2)}) async-start(), calls=%async_computation.10 | async-start | bytes 10485760 | tf_op jit(solution)/shard_map/all_gather | solution.py:480
  426.6 268.4 %all-gather.20.cloned.1.call-start = ((), (), s32[]{:S(2)}) async-start(), calls=%async_computation.11 | async-start | bytes 10485760 | tf_op jit(solution)/shard_map/all_gather | solution.py:480
  548.3 59.6 %all-to-all-start.2 = ((bf16[4,1024,512]{2,1,0:T(8,128)(2,1)}), bf16[4,1024,512]{2,1,0:T(8,128)(2,1)}, u32[]{:S(2)}, u32[]{:S(2)}) async-start(bf16[4,1024,512]{2,1,0:T(8,128)(2,1)} %bitcast.134), calls=%async_computation.2 | async-start | bytes 8388608 | tf_op jit(solution)/shard_map/all_to_all | solution.py:483
  607.9 5.5 copy-start.9
  607.9 5.5 copy-start.10
  607.9 53.2 %all-to-all-start.3 = ((bf16[4,1024,512]{2,1,0:T(8,128)(2,1)}), bf16[4,1024,512]{2,1,0:T(8,128)(2,1)}, u32[]{:S(2)}, u32[]{:S(2)}) async-start(bf16[4,1024,512]{2,1,0:T(8,128)(2,1)} %bitcast.135), calls=%async_computation.3 | async-start | bytes 8388608 | tf_op jit(solution)/shard_map/all_to_all | solution.py:483
  612.9 135.9 %all-gather.22.cloned.1.call-start = ((), (), s32[]{:S(2)}) async-start(), calls=%async_computation.12 | async-start | bytes 10485760 | tf_op jit(solution)/shard_map/all_gather | solution.py:480
  802.4 53.2 %all-to-all-start.4 = ((bf16[4,1024,512]{2,1,0:T(8,128)(2,1)}), bf16[4,1024,512]{2,1,0:T(8,128)(2,1)}, u32[]{:S(2)}, u32[]{:S(2)}) async-start(bf16[4,1024,512]{2,1,0:T(8,128)(2,1)} %bitcast.133), calls=%async_computation.4 | async-start | bytes 8388608 | tf_op jit(solution)/shard_map/all_to_all | solution.py:483
  855.6 52.5 %all-to-all-start.7 = ((f32[4,2,2048]{2,1,0:T(2,128)}), f32[4,2,2048]{2,1,0:T(2,128)S(1)}, u32[]{:S(2)}, u32[]{:S(2)}) async-start(f32[4,2,2048]{2,1,0:T(2,128)} %copy.143), calls=%async_computation.7 | async-start | bytes 131072 | tf_op jit(solution)/shard_map/all_to_all | solution.py:510
  908.1 90.8 %all-to-all-start.5 = ((bf16[4,1024,512]{2,1,0:T(8,128)(2,1)}), bf16[4,1024,512]{2,1,0:T(8,128)(2,1)}, u32[]{:S(2)}, u32[]{:S(2)}) async-start(bf16[4,1024,512]{2,1,0:T(8,128)(2,1)} %bitcast.130), calls=%async_computation.5 | async-start | bytes 8388608 | tf_op jit(solution)/shard_map/all_to_all | solution.py:483
  913.2 33.1 %copy-start.2 = (s32[2048,2]{0,1:T(2,128)S(1)}, s32[2048,2]{0,1:T(2,128)}, u32[]{:S(2)}) copy-start(s32[2048,2]{0,1:T(2,128)} %param.22) | copy-start | bytes 49156
  913.2 33.7 %copy-start.7 = (f32[4,2048]{1,0:T(4,128)S(1)}, f32[4,2048]{1,0:T(4,128)}, u32[]{:S(2)}) copy-start(f32[4,2048]{1,0:T(4,128)} %get-tuple-element.109) | copy-start | bytes 98308
  913.2 33.7 %copy-start.8 = (f32[4,2048]{1,0:T(4,128)S(1)}, f32[4,2048]{1,0:T(4,128)}, u32[]{:S(2)}) copy-start(f32[4,2048]{1,0:T(4,128)} %get-tuple-element.113) | copy-start | bytes 98308
  999.6 15.6 %all-to-all-start.6 = ((f32[4,2,2048]{2,1,0:T(2,128)}), f32[4,2,2048]{2,1,0:T(2,128)S(1)}, u32[]{:S(2)}, u32[]{:S(2)}) async-start(f32[4,2,2048]{2,1,0:T(2,128)} %copy.142), calls=%async_computation.6 | async-start | bytes 131072 | tf_op jit(solution)/shard_map/all_to_all | solution.py:510
  1002.9 12.4 %copy-start.4 = (s32[2048,2]{0,1:T(2,128)S(1)}, s32[2048,2]{0,1:T(2,128)}, u32[]{:S(2)}) copy-start(s32[2048,2]{0,1:T(2,128)} %param.20) | copy-start | bytes 49156
Sparse Core Ops, SparseCore 0:
  9.5 59.1 all-gather.13
  71.1 88.2 all-gather.27
  162.2 107.7 all-gather.23
  272.6 69.5 all-gather.25
  344.1 56.3 all-gather.15
  426.7 56.5 all-gather.17
  484.8 56.4 all-gather.19
  694.4 54.4 all-gather.21
